TPU v7x, 128 devices: a whole 4x4x4 slice. The times are simulated.
128 devices in a mesh: seq: 16 (over x_hi, y, core), head: 8 (over z, x_lo).
Axes of the slice: x: 4 (x_hi: 2, x_lo: 2; x = x_hi * 2 + x_lo), y: 4, z: 4, core: 2. Of those that a mesh axis runs over, the one named last changes fastest.
Arguments:
- mid: bfloat16 [4096, 3072], P('seq'), may hold values from -20 to 20
- second_in: bfloat16 [4096, 3072], P('seq'), may hold values from -20 to 20
- cotangent: bfloat16 [4096, 3072], P('seq'), may hold values from -6 to 6
- w_key: bfloat16 [3072, 1024], P(None, 'head'), may hold values from -0.109375 to 0.109375
- w_value: bfloat16 [3072, 1024], P(None, 'head'), may hold values from -0.109375 to 0.109375
- w_query: bfloat16 [2, 3072, 3072], P(None, None, 'head'), may hold values from -0.109375 to 0.109375
- w_out: bfloat16 [2, 3072, 3072], P(None, 'head'), may hold values from -0.109375 to 0.109375
- w_ret_out: bfloat16 [3072, 3072], P('head'), may hold values from -0.109375 to 0.109375
- ret_query: bfloat16 [4096, 3072], P('seq', 'head'), may hold values from -6 to 6
- ret_key: bfloat16 [4096, 3072], P('seq', 'head'), may hold values from -3 to 3
- ret_value: bfloat16 [4096, 3072], P('seq', 'head'), may hold values from -6 to 6
- gate: float32 [24, 4096], P('head', 'seq'), may hold values from 0 to 6
- decay_exp: int32 [24], P('head'), may hold values from 0 to 256
- mask_start: int32 [32], P('seq'), may hold values from 0 to 3968, as said below
Outputs:
- grad_mid: bfloat16 [4096, 3072], P('seq')
- grad_ret_query: bfloat16 [4096, 3072], P('seq', 'head')
- grad_ret_key: bfloat16 [4096, 3072], P('seq', 'head')
- grad_ret_value: bfloat16 [4096, 3072], P('seq', 'head')
- grad_w_key: float32 [3072, 1024], P(None, 'head')
- grad_w_value: float32 [3072, 1024], P(None, 'head')
Inputs may be any that keep to these rules, and one draw needn't show every extreme that they name: `mask_start`: the entry of each block of 128 queries is at most the position of that block's first query.
All inputs are finite; a program needn't handle non-finite values.
Results may differ from a plain program's by a relative error of at most 0.025.
The roundings to bfloat16 on the way count: a program that leaves them out, or rounds other values in their place, can miss the bound.
Values may be sent and summed in bfloat16 or wider, within the bound.
A program may use at most 192 MiB of HBM per device.

v0:
```python
import functools
import math

import jax
import jax.numpy as jnp
from jax import lax
from jax.experimental import pallas as pl
from jax.experimental.pallas import tpu as pltpu
from jax.sharding import Mesh
from jax.sharding import PartitionSpec as P

E = 128
BLK = 128
RC = 128
SEQ = ("xh", "y", "core")
HEAD = ("z", "xl")

MESH = pl.DeviceIdType.MESH
BF16 = jnp.bfloat16
F32 = jnp.float32


class Wire:
    def __init__(self, send, recv):
        self.send, self.recv, self.sent, self.used = send, recv, [], 0

    def put(self, src, dst, to):
        k = self.used
        self.used += 1
        copy = pltpu.make_async_remote_copy(
            src_ref=src,
            dst_ref=dst,
            send_sem=self.send.at[k],
            recv_sem=self.recv.at[k],
            device_id=to,
            device_id_type=MESH,
        )
        copy.start()
        self.sent.append(copy)
        return (k, to)

    def got(self, ticket, landed):
        k, to = ticket
        pltpu.make_async_remote_copy(
            src_ref=landed,
            dst_ref=landed,
            send_sem=self.send.at[k],
            recv_sem=self.recv.at[k],
            device_id=to,
            device_id_type=MESH,
        ).wait_recv()

    def drain(self):
        for copy in self.sent:
            copy.wait_send()


def meet(peers):
    barrier = pltpu.get_barrier_semaphore()
    for to in peers:
        pl.semaphore_signal(barrier, inc=1, device_id=to, device_id_type=MESH)
    pl.semaphore_wait(barrier, len(peers))


def near(axis):
    at = lax.axis_index(axis)
    return at, lax.rem(at + 1, 4), lax.rem(at + 3, 4), lax.rem(at + 2, 4)


def seq_peers():
    y, yp, ym, y2 = near("y")
    return [
        {"xh": 1 - lax.axis_index("xh")},
        {"y": yp},
        {"y": ym},
        {"core": 1 - lax.axis_index("core")},
    ]


def head_peers():
    z, zp, zm, z2 = near("z")
    return [{"xl": 1 - lax.axis_index("xl")}, {"z": zp}, {"z": zm}]


def by_rows(ref, rows, parts=2):
    step = rows // parts

    def at(slot, first, count):
        return ref.at[pl.ds(pl.multiple_of(slot * rows + first, step), count)]

    return at


def by_columns(ref, width):
    def at(slot, first, count):
        return ref.at[pl.ds(first, count), pl.ds(pl.multiple_of(slot * width, 128), width)]

    return at


def add_to(total, part):
    total[...] = (total[...].astype(F32) + part[...].astype(F32)).astype(total.dtype)


def together(*runs):
    runs = list(runs)
    while runs:
        for run in list(runs):
            try:
                next(run)
            except StopIteration:
                runs.remove(run)
        yield


def finish(run):
    for _ in run:
        pass


def gather_seq(wire, at, rows):
    xh, c = lax.axis_index("xh"), lax.axis_index("core")
    y, yp, ym, y2 = near("y")
    xo, co = 1 - xh, 1 - c
    half = rows // 2
    whole, low, high = (0, rows), (0, half), (half, half)
    across, up, down, beside = {"xh": xo}, {"y": yp}, {"y": ym}, {"core": co}

    def slot(a, b, d):
        return a * 8 + b * 2 + d

    def pass_on(s, part, to):
        return wire.put(at(s, *part), at(s, *part), to)

    side = []
    own, far = slot(xh, y, c), slot(xo, y, c)
    t_x = pass_on(own, whole, across)
    ups, downs = [pass_on(own, whole, up)], [pass_on(own, whole, down)]
    side.append((pass_on(own, whole, beside), slot(xh, y, co)))
    yield
    wire.got(t_x, at(far, *whole))
    ups.append(pass_on(far, whole, up))
    downs.append(pass_on(far, whole, down))
    side.append((pass_on(far, whole, beside), slot(xo, y, co)))
    yield
    last = []
    for k, q in enumerate((xh, xo)):
        wire.got(ups[k], at(slot(q, ym, c), *whole))
        a = pass_on(slot(q, ym, c), low, up)
        side.append((pass_on(slot(q, ym, c), whole, beside), slot(q, ym, co)))
        wire.got(downs[k], at(slot(q, yp, c), *whole))
        b = pass_on(slot(q, yp, c), high, down)
        side.append((pass_on(slot(q, yp, c), whole, beside), slot(q, yp, co)))
        last.append((a, b))
        yield
    for k, q in enumerate((xh, xo)):
        wire.got(last[k][0], at(slot(q, y2, c), *low))
        wire.got(last[k][1], at(slot(q, y2, c), *high))
        side.append((pass_on(slot(q, y2, c), whole, beside), slot(q, y2, co)))
        yield
    for ticket, s in side:
        wire.got(ticket, at(s, *whole))


def ring_scatter(wire, at, slot, axis, first, count, land, before=None):
    r, rp, rm, r2 = near(axis)
    up, down = {axis: rp}, {axis: rm}
    half = count // 2
    wait = before or (lambda j: None)
    low, high = land.at[pl.ds(0, half)], land.at[pl.ds(half, half)]
    from_up, from_down = land.at[pl.ds(count, count)], land.at[pl.ds(2 * count, count)]
    wait(2)
    a = wire.put(at(slot(r2), first, half), low, up)
    b = wire.put(at(slot(r2), first + half, half), high, down)
    yield
    wait(1)
    wire.got(a, low)
    add_to(at(slot(rp), first, half), low)
    u = wire.put(at(slot(rp), first, count), from_down, up)
    wait(3)
    wire.got(b, high)
    add_to(at(slot(rm), first + half, half), high)
    d = wire.put(at(slot(rm), first, count), from_up, down)
    yield
    wait(0)
    wire.got(u, from_down)
    add_to(at(slot(r), first, count), from_down)
    wire.got(d, from_up)
    add_to(at(slot(r), first, count), from_up)


def scatter_seq(wire, at, rows, land):
    xh, c = lax.axis_index("xh"), lax.axis_index("core")
    y, yp, ym, y2 = near("y")
    xo, co = 1 - xh, 1 - c

    def slot(a, b, d):
        return a * 8 + b * 2 + d

    def block(k, count=1):
        return land.at[pl.ds(k * rows, count * rows)]

    places = {0: y, 1: yp, 2: y2, 3: ym}
    side = {}
    for n, q in enumerate((xo, xh)):
        for m, j in enumerate((2, 1, 3, 0)):
            dst = block(4 * n + m)
            side[n, j] = (wire.put(at(slot(q, places[j], co), 0, rows), dst, {"core": co}), dst)

    def before(n, q):
        def wait(j):
            ticket, dst = side[n, j]
            wire.got(ticket, dst)
            add_to(at(slot(q, places[j], c), 0, rows), dst)

        return wait

    def ring(n, q):
        return ring_scatter(
            wire, at, lambda j: slot(q, j, c), "y", 0, rows, block(8 + 3 * n, 3), before(n, q)
        )

    sent = []

    def far():
        yield from ring(0, xo)
        sent.append(wire.put(at(slot(xo, y, c), 0, rows), block(14), {"xh": xo}))

    yield from together(far(), ring(1, xh))
    wire.got(sent[0], block(14))
    return block(14)


def scatter_head(wire, at, rows, land):
    xl = lax.axis_index("xl")
    z, zp, zm, z2 = near("z")
    xo = 1 - xl
    half = rows // 2

    def slot(j, q):
        return j * 2 + q

    def block(k, count=1):
        return land.at[pl.ds(k * half, count * half)]

    places = {0: z, 1: zp, 2: z2, 3: zm}
    side = {}
    for m, j in enumerate((2, 1, 3, 0)):
        side[j] = (wire.put(at(slot(places[j], xo), 0, half), block(m), {"xl": xo}), block(m))

    def wait(j):
        ticket, dst = side[j]
        wire.got(ticket, dst)
        add_to(at(slot(places[j], xl), 0, half), dst)

    sent = []

    def far():
        yield from ring_scatter(
            wire, at, lambda j: slot(j, xo), "z", half, half, block(4, 3)
        )
        sent.append(wire.put(at(slot(z, xo), half, half), block(13), {"xl": xo}))

    yield from together(
        far(),
        ring_scatter(wire, at, lambda j: slot(j, xl), "z", half, half, block(7, 3)),
        ring_scatter(wire, at, lambda j: slot(j, xl), "z", 0, half, block(10, 3), wait),
    )
    wire.got(sent[0], block(13))
    add_to(at(slot(z, xl), half, half), block(13))


def gather_head(wire, at, rows):
    xl = lax.axis_index("xl")
    z, zp, zm, z2 = near("z")
    xo = 1 - xl
    half = rows // 2
    up, down, across = {"z": zp}, {"z": zm}, {"xl": xo}

    def slot(j, q):
        return j * 2 + q

    def pass_on(s, first, count, to):
        return wire.put(at(s, first, count), at(s, first, count), to)

    def ring(q, first, each=None):
        h = half // 2
        tell = each or (lambda j: None)
        a = pass_on(slot(z, q), first, half, up)
        b = pass_on(slot(z, q), first, half, down)
        tell(z)
        yield
        wire.got(a, at(slot(zm, q), first, half))
        c = pass_on(slot(zm, q), first, h, up)
        tell(zm)
        wire.got(b, at(slot(zp, q), first, half))
        d = pass_on(slot(zp, q), first + h, h, down)
        tell(zp)
        yield
        wire.got(c, at(slot(z2, q), first, h))
        wire.got(d, at(slot(z2, q), first + h, h))
        tell(z2)

    side = []

    def tell(j):
        side.append((pass_on(slot(j, xl), 0, half, across), slot(j, xo)))

    t_x = pass_on(slot(z, xl), half, half, across)

    def far():
        wire.got(t_x, at(slot(z, xo), half, half))
        yield from ring(xo, half)

    yield from together(ring(xl, 0, tell), ring(xl, half), far())
    for ticket, s in side:
        wire.got(ticket, at(s, 0, half))


ANY = pl.BlockSpec(memory_space=pl.ANY)
VMEM = pl.BlockSpec(memory_space=pltpu.VMEM)


def wires(count):
    return [pltpu.SemaphoreType.DMA((count,)), pltpu.SemaphoreType.DMA((count,))]


def params(number):
    return pltpu.CompilerParams(collective_id=number, has_side_effects=True)


def bring(*pairs, sem):
    copies = [pltpu.make_async_copy(s, d, sem.at[k]) for k, (s, d) in enumerate(pairs)]
    for copy in copies:
        copy.start()
    return copies


def seq_index():
    return lax.axis_index("xh") * 8 + lax.axis_index("y") * 2 + lax.axis_index("core")


def head_index():
    return lax.axis_index("z") * 2 + lax.axis_index("xl")


def total_into(out_at, acc_at, residual, rows, width):
    me = head_index()
    own = acc_at(me, 0, rows)
    kept = residual.at[pl.ds(0, rows), pl.ds(pl.multiple_of(me * width, 128), width)]
    out_at(me, 0, rows)[...] = (kept[...].astype(F32) + own[...].astype(F32)).astype(BF16)


def head_run(wire, acc, land, residual, out):
    rows, columns = acc.shape
    width = columns // 8
    yield from scatter_head(wire, by_columns(acc, width), rows, land)
    total_into(by_columns(out, width), by_columns(acc, width), residual, rows, width)
    yield from gather_head(wire, by_columns(out, width), rows)


def upstream_kernel(
    part, residual, state, decay, out, states, decays, acc, land, local, send, recv
):
    s_rows, d_rows = state.shape[0], decay.shape[0]
    s_at, d_at = by_rows(states, s_rows), by_rows(decays, d_rows)
    me = seq_index()
    copies = bring(
        (part, acc), (state, s_at(me, 0, s_rows)), (decay, d_at(me, 0, d_rows)), sem=local
    )
    meet(seq_peers() + head_peers())
    for copy in copies:
        copy.wait()
    wire = Wire(send, recv)
    finish(
        together(
            head_run(wire, acc, land, residual, out),
            gather_seq(wire, s_at, s_rows),
            gather_seq(wire, d_at, d_rows),
        )
    )
    wire.drain()


def upstream_of(part, residual, state, decay, number):
    rows, columns = part.shape
    return pl.pallas_call(
        upstream_kernel,
        out_shape=(
            jax.ShapeDtypeStruct(part.shape, BF16),
            jax.ShapeDtypeStruct((16 * state.shape[0], state.shape[1]), BF16),
            jax.ShapeDtypeStruct((16 * decay.shape[0], decay.shape[1]), F32),
        ),
        in_specs=[ANY, VMEM, ANY, ANY],
        out_specs=(VMEM, VMEM, VMEM),
        scratch_shapes=[
            pltpu.VMEM(part.shape, BF16),
            pltpu.VMEM((7 * rows, columns // 8), BF16),
            pltpu.SemaphoreType.DMA((3,)),
            *wires(90),
        ],
        compiler_params=params(number),
    )(part, residual, state, decay)


def dot_last(a, b):
    return lax.dot_general(a, b, (((1,), (1,)), ((), ())), preferred_element_type=F32)


def dot(a, b):
    return jnp.dot(a, b, preferred_element_type=F32)


def folded(value, op):
    parts = [value[:, k : k + 128] for k in range(0, value.shape[1], 128)]
    while len(parts) > 1:
        parts = [op(a, b) for a, b in zip(parts[::2], parts[1::2])]
    return parts[0]


CHUNK = 512


def fill_bias(bias, firsts, position, rows, length):
    row = lax.broadcasted_iota(jnp.int32, (rows, CHUNK), 0)
    low = jnp.where(row < BLK, firsts[0], firsts[1])
    high = row + position
    for k in range(0, length, CHUNK):
        column = lax.broadcasted_iota(jnp.int32, (rows, CHUNK), 1) + k
        seen = (column >= low) & (column <= high)
        bias[:, k : k + CHUNK] = jnp.where(seen, 0.0, -jnp.inf)


def one_head(q, g, kv, bias, raised, rounded, total, first):
    length = kv.shape[0]
    rows = q.shape[0]
    factor = 1.0 / math.sqrt(E)
    chunks = [slice(k, k + CHUNK) for k in range(0, length, CHUNK)]
    top = None
    for k in chunks:
        scores = dot_last(q, kv[k, :E]) + bias[:, k]
        raised[:, k] = scores
        most = folded(scores, jnp.maximum)
        top = most if top is None else jnp.maximum(top, most)
    top = jnp.max(top, axis=1, keepdims=True)
    whole = None
    for k in chunks:
        power = jnp.exp2((raised[:, k] - top) * (factor * math.log2(math.e)))
        raised[:, k] = power
        part = folded(power, jnp.add)
        whole = part if whole is None else whole + part
    inverse = 1.0 / jnp.sum(whole, axis=1, keepdims=True)
    outputs = jnp.zeros((rows, E), F32)
    for k in chunks:
        near_probs = (raised[:, k] * inverse).astype(BF16)
        rounded[:, k] = near_probs
        outputs = outputs + dot(near_probs, kv[k, E:])
    outputs = outputs.astype(BF16).astype(F32)
    delta = jnp.sum(g.astype(F32) * outputs, axis=1, keepdims=True)
    scaled = inverse * factor
    q_t = q.astype(F32).T.astype(BF16)
    g_t = g.astype(F32).T.astype(BF16)
    query_grad = jnp.zeros((rows, E), F32)
    for k in chunks:
        dprobs = dot_last(g, kv[k, E:])
        dscores = ((raised[:, k] * scaled) * (dprobs - delta)).astype(BF16)
        query_grad = query_grad + dot(dscores, kv[k, :E])
        total[:E, k] = total[:E, k] + dot(q_t, dscores)
        total[E:, k] = total[E:, k] + dot(g_t, rounded[:, k])
    return query_grad.astype(BF16)


def attend_kernel(firsts, q, g, kv, before, q_grad, after, bias, raised, rounded):
    rows, length = q.shape[0], kv.shape[0]
    fill_bias(bias, firsts, seq_index() * rows, rows, length)
    if before is None:
        after[...] = jnp.zeros_like(after)
    else:
        after[...] = before[...]

    def head(h, _):
        at = pl.ds(pl.multiple_of(h * E, E), E)
        q_grad[:, at] = one_head(q[:, at], g[:, at], kv, bias, raised, rounded, after, h)
        return 0

    lax.fori_loop(0, q.shape[1] // E, head, 0)


def attend(queries, grad_out, kv, firsts, before, final):
    rows, width = queries.shape
    length = kv.shape[0]
    kept = BF16 if final else F32
    operands = [firsts, queries, grad_out, kv]
    specs = [pl.BlockSpec(memory_space=pltpu.SMEM), VMEM, VMEM, VMEM]
    if before is not None:
        operands.append(before)
        specs.append(VMEM)

    def kernel(*refs):
        ins, rest = list(refs[: len(operands)]), refs[len(operands) :]
        if before is None:
            ins.append(None)
        q_grad, after, total, bias, raised, rounded = rest
        attend_kernel(*ins, q_grad, total, bias, raised, rounded)
        after[...] = total[...].astype(kept)

    return pl.pallas_call(
        kernel,
        out_shape=(
            jax.ShapeDtypeStruct((rows, width), BF16),
            jax.ShapeDtypeStruct((2 * E, length), kept),
        ),
        in_specs=specs,
        out_specs=(VMEM, VMEM),
        scratch_shapes=[
            pltpu.VMEM((2 * E, length), F32),
            pltpu.VMEM((rows, length), F32),
            pltpu.VMEM((rows, length), F32),
            pltpu.VMEM((rows, length), BF16),
        ],
        compiler_params=pltpu.CompilerParams(vmem_limit_bytes=56 * 1024 * 1024),
    )(*operands)


def weave(run, work, steps):
    work = list(work)
    each = -(-len(work) // steps)
    for _ in run:
        for item in work[:each]:
            item()
        work = work[each:]
    for item in work:
        item()


def flipped(value):
    return value.astype(F32).T


def log_decays(logs):
    t = lax.broadcasted_iota(jnp.int32, (RC, RC), 0)
    s = lax.broadcasted_iota(jnp.int32, (RC, RC), 1)
    upto = jnp.where(t <= s, 1.0, 0.0)
    rows, columns = [], []
    for c in range(logs.shape[1] // RC):
        part = jnp.dot(
            logs[:, c * RC : (c + 1) * RC],
            upto,
            precision=lax.Precision.HIGHEST,
            preferred_element_type=F32,
        )
        rows.append(part)
        tall = jnp.concatenate((part, jnp.zeros((RC - part.shape[0], RC), F32)), axis=0)
        columns.append(tall.T)
    return rows, columns


def spread(peers):
    z, xl = lax.axis_index("z"), lax.axis_index("xl")
    places = []
    for k in range(1, 8):
        to = (lax.rem(z + k // 2, 4), lax.rem(xl + k, 2))
        came = (lax.rem(z + 4 - k // 2, 4), lax.rem(xl + k, 2))
        places.append((to, came))
    return places


def open_kernel(
    mid_in, second_in, cot_in, wk_in, wv_in, wq_in, wo_in, ret_key, ret_value, logs,
    kv, q1, g1, q0, mid_t, slices, first_state, state, decay,
    mid, second, cot, wkv, wq1, wo1, wq0, flip, kept, local, sent, send, recv,
):
    rows = mid.shape[0]
    share = wkv.shape[0] // 8
    me = head_index()
    copies = bring(
        (mid_in, mid),
        (wk_in, wkv.at[:, pl.ds(0, E)]),
        (wv_in, wkv.at[:, pl.ds(E, E)]),
        (second_in, second),
        (wq_in.at[1], wq1),
        (cot_in, cot),
        (wo_in.at[1], wo1),
        (wq_in.at[0], wq0),
        sem=local,
    )
    places = spread(7)
    meet(seq_peers() + [{"z": a, "xl": b} for (a, b), _ in places])
    for copy in copies[:3]:
        copy.wait()
    wire = Wire(send, recv)
    at = by_rows(kv, rows)
    at(seq_index(), 0, rows)[...] = dot(mid[...], wkv[...]).astype(BF16)
    own = pltpu.make_async_copy(
        wkv.at[pl.ds(pl.multiple_of(me * share, share), share)], kept.at[me], sent.at[0]
    )
    own.start()

    def exchange():
        tickets = []
        for (a, b), (ca, cb) in places:
            src = wkv.at[pl.ds(pl.multiple_of((a * 2 + b) * share, share), share)]
            tickets.append((wire.put(src, kept.at[me], {"z": a, "xl": b}), ca * 2 + cb))
        yield
        yield
        yield
        yield
        yield
        for ticket, slot in tickets:
            wire.got(ticket, kept.at[slot])

    work = []

    def product(out, left, right, how, number):
        def first():
            copies[number].wait()
            if number != 7:
                copies[number - 1].wait()
            out[:, : 2 * E] = how(left, right, 0, 2 * E).astype(BF16)

        def rest():
            out[:, 2 * E :] = how(left, right, 2 * E, E).astype(BF16)

        work.extend((first, rest))

    def straight(left, right, at, count):
        return dot(left[...], right[:, at : at + count])

    def across(left, right, at, count):
        return dot_last(left[...], right[at : at + count])

    product(q1, second, wq1, straight, 4)
    product(g1, cot, wo1, across, 6)
    product(q0, mid, wq0, straight, 7)

    def states():
        arow, acol = log_decays(logs[...])
        total = arow[0][:, RC - 1 :] + arow[1][:, RC - 1 :]
        decay[:8] = jnp.broadcast_to(total, (8, 128))
        decay[8:] = jnp.zeros((8, 128), F32)
        for r in range(ret_key.shape[1] // E):
            cols = slice(r * E, (r + 1) * E)
            made = []
            for c in range(2):
                span = slice(c * RC, (c + 1) * RC)
                shrink = jnp.exp(arow[c][r : r + 1, RC - 1 :] - acol[c][:, r : r + 1])
                scaled = (shrink * ret_key[span, cols].astype(F32)).astype(BF16)
                made.append(dot(flipped(scaled).astype(BF16), ret_value[span, cols]))
            first_state[cols] = made[0]
            last = jnp.exp(arow[1][r : r + 1, RC - 1 :])
            state[cols] = (last * made[0] + made[1]).astype(BF16)

    work.append(states)

    def turn(k):
        def go():
            for j in range(k, k + 512, 128):
                flip[j : j + 128] = flipped(mid[:, j : j + 128]).astype(BF16)

        return go

    work.extend(turn(k) for k in range(0, mid.shape[1], 512))
    weave(together(gather_seq(wire, at, rows), exchange()), work, 6)
    own.wait()
    outs = [
        pltpu.make_async_copy(flip, mid_t, sent.at[1]),
        pltpu.make_async_copy(kept, slices, sent.at[2]),
    ]
    for copy in outs:
        copy.start()
    wire.drain()
    for copy in outs:
        copy.wait()


def open_stage(mid, second_in, cot, w_key, w_value, w_query, w_out, ret_key, ret_value, logs, number):
    rows, depth = mid.shape
    wide = w_query.shape[2]
    shape = jax.ShapeDtypeStruct
    return pl.pallas_call(
        open_kernel,
        out_shape=(
            shape((16 * rows, 2 * E), BF16),
            shape((rows, wide), BF16),
            shape((rows, wide), BF16),
            shape((rows, wide), BF16),
            shape((depth, rows), BF16),
            shape((8, depth // 8, 2 * E), BF16),
            shape((wide, E), F32),
            shape((wide, E), BF16),
            shape((16, 128), F32),
        ),
        in_specs=[ANY] * 7 + [VMEM] * 3,
        out_specs=(VMEM, VMEM, VMEM, VMEM, ANY, ANY, VMEM, VMEM, VMEM),
        scratch_shapes=[
            pltpu.VMEM((rows, depth), BF16),
            pltpu.VMEM((rows, depth), BF16),
            pltpu.VMEM((rows, depth), BF16),
            pltpu.VMEM((depth, 2 * E), BF16),
            pltpu.VMEM((depth, wide), BF16),
            pltpu.VMEM((wide, depth), BF16),
            pltpu.VMEM((depth, wide), BF16),
            pltpu.VMEM((depth, rows), BF16),
            pltpu.VMEM((8, depth // 8, 2 * E), BF16),
            pltpu.SemaphoreType.DMA((8,)),
            pltpu.SemaphoreType.DMA((3,)),
            *wires(30),
        ],
        compiler_params=params(number),
    )(mid, second_in, cot, w_key, w_value, w_query, w_out, ret_key, ret_value, logs)


def close_kernel(
    part_in, res_in, dkv_in, slices_in, mid_t_in, w_ret_in, states_in,
    rq, rk, rv, logs, decays, first_state,
    grad_mid, gq, gk, gv, gwk, gwv,
    acc_m, land_m, acc_k, land_k, kv_all, w_acc, w_land, w_sum, grads,
    residual, slices, mid_t, w_ret, states, local, send, recv,
):
    rows, depth = acc_m.shape
    share = depth // 8
    heads = rq.shape[1] // E
    me, here = head_index(), seq_index()
    copies = bring(
        (dkv_in, acc_k),
        (part_in, acc_m),
        (mid_t_in, mid_t),
        (slices_in, slices),
        (res_in, residual),
        (w_ret_in, w_ret),
        (states_in, states),
        sem=local,
    )
    meet(seq_peers() + head_peers())
    copies[0].wait()
    copies[1].wait()
    wire = Wire(send, recv)
    kv_at = by_rows(kv_all, rows, 4)
    w_rows = depth // 16
    w_at = by_rows(w_sum, w_rows)
    s_rows = heads * E
    s_at = by_rows(grads, s_rows)
    arow, acol = log_decays(logs[...])
    t = lax.broadcasted_iota(jnp.int32, (RC, RC), 0)
    s = lax.broadcasted_iota(jnp.int32, (RC, RC), 1)
    pieces = [(r, c) for r in range(heads) for c in range(2)]
    where = {(r, c): (slice(c * RC, (c + 1) * RC), slice(r * E, (r + 1) * E)) for r, c in pieces}
    weights, second, turned, entering, after = {}, {}, {}, {}, {}

    def end(r, c):
        return arow[c][r : r + 1, RC - 1 :]

    def prepare(r, c):
        a_t, a_s = acol[c][:, r : r + 1], arow[c][r : r + 1]
        lower = t >= s
        weights[r, c] = jnp.where(lower, jnp.exp(jnp.where(lower, a_t - a_s, 0.0)), 0.0)
        q, k = rq[where[r, c]], rk[where[r, c]]
        both = (weights[r, c] * dot_last(q, k)).astype(BF16)
        second[r, c] = flipped(both).astype(BF16)
        grown = (jnp.exp(a_t) * q.astype(F32)).astype(BF16)
        turned[r, c] = flipped(grown).astype(BF16)

    def arriving(r):
        cols = where[r, 0][1]
        now = jnp.zeros((E, E), F32)
        for k in range(15):
            mine = states[k * s_rows + r * E : k * s_rows + (r + 1) * E].astype(F32)
            new = jnp.exp(decays[k * 16 + r : k * 16 + r + 1]) * now + mine
            now = jnp.where(k < here, new, now)
        entering[r, 0] = now.astype(BF16)
        entering[r, 1] = (jnp.exp(end(r, 0)) * now + first_state[cols]).astype(BF16)

    def early():
        copies[6].wait()

    work = [early]
    for r in range(heads):
        work.append(lambda r=r: arriving(r))
    for r, c in pieces:
        work.append(lambda r=r, c=c: prepare(r, c))

    def keys():
        at = by_columns(acc_k, rows)
        rest = yield from scatter_seq(wire, at, rows, land_k)
        own = at(here, 0, rows)
        total = own[...].astype(F32) + rest[...].astype(F32)
        kv_at(me, 0, rows)[...] = total.T.astype(BF16)

    m_at = by_columns(acc_m, share)
    weave(together(keys(), scatter_head(wire, m_at, rows, land_m)), work, 3)
    own_kv = kv_at(me, 0, rows)
    gather_kv = gather_head(wire, kv_at, rows)
    next(gather_kv)
    copies[2].wait()
    w_acc[...] = dot(mid_t[...], own_kv[...]).astype(BF16)

    def sums():
        at = by_rows(w_acc, w_rows)
        rest = yield from scatter_seq(wire, at, w_rows, w_land)
        w_at(here, 0, w_rows)[...] = (
            at(here, 0, w_rows)[...].astype(F32) + rest[...].astype(F32)
        ).astype(BF16)
        yield
        yield from gather_seq(wire, w_at, w_rows)

    shared = sums()
    next(shared)
    finish(gather_kv)
    copies[3].wait()
    copies[4].wait()
    total = m_at(me, 0, rows)[...].astype(F32)
    total = total + residual[:, pl.ds(pl.multiple_of(me * share, 128), share)].astype(F32)
    for h in range(8):
        total = total + dot_last(kv_at(h, 0, rows)[...], slices[h])
    out_at = by_columns(grad_mid, share)
    out_at(me, 0, rows)[...] = total.astype(BF16)

    def beside(run):
        for _ in run:
            next(shared, None)

    beside(gather_head(wire, out_at, rows))
    copies[5].wait()
    grad_o = dot_last(grad_mid[...], w_ret[...]).astype(BF16)
    own_grad = {}
    for r, c in pieces:
        span, cols = where[r, c]
        own_grad[r, c] = dot(turned[r, c], grad_o[span, cols]) * (1.0 / E)
    for r in range(heads):
        made = own_grad[r, 0] + jnp.exp(end(r, 0)) * own_grad[r, 1]
        grads[pl.ds(pl.multiple_of(here * s_rows + r * E, E), E)] = made.astype(BF16)
    back = gather_seq(wire, s_at, s_rows)
    next(back)
    inner = {}

    def inside(r, c):
        span, cols = where[r, c]
        g, q, k, v = grad_o[span, cols], rq[span, cols], rk[span, cols], rv[span, cols]
        first = (weights[r, c] * dot_last(g, v)).astype(BF16)
        grow = jnp.exp(acol[c][:, r : r + 1])
        carried = grow * dot_last(g, entering[r, c])
        gq[span, cols] = ((dot(first, k) + carried) * (1.0 / E)).astype(BF16)
        inner[r, c] = (
            dot(flipped(first).astype(BF16), q) * (1.0 / E),
            dot(second[r, c], g) * (1.0 / E),
        )

    work = [lambda r=r, c=c: inside(r, c) for r, c in pieces]

    def both():
        for _ in back:
            next(shared, None)
            yield

    weave(both(), work, 5)
    for r in range(heads):
        now = jnp.zeros((E, E), F32)
        for k in range(15, 0, -1):
            mine = grads[k * s_rows + r * E : k * s_rows + (r + 1) * E].astype(F32)
            new = mine + jnp.exp(decays[k * 16 + r : k * 16 + r + 1]) * now
            now = jnp.where(k > here, new, now)
        after[r, 1] = now.astype(BF16)
        after[r, 0] = (own_grad[r, 1] + jnp.exp(end(r, 1)) * now).astype(BF16)
    for r, c in pieces:
        span, cols = where[r, c]
        shrink = jnp.exp(end(r, c) - acol[c][:, r : r + 1])
        gk[span, cols] = (
            inner[r, c][0] + shrink * dot_last(rv[span, cols], after[r, c])
        ).astype(BF16)
        gv[span, cols] = (inner[r, c][1] + shrink * dot(rk[span, cols], after[r, c])).astype(BF16)
    finish(shared)
    gwk[...] = w_sum[:, :E].astype(F32)
    gwv[...] = w_sum[:, E:].astype(F32)
    wire.drain()


def close_stage(
    part, residual, dkv, slices, mid_t, w_ret, states, rq, rk, rv, logs, decays, first_state, number
):
    rows, depth = part.shape
    width = rq.shape[1]
    shape = jax.ShapeDtypeStruct
    return pl.pallas_call(
        close_kernel,
        out_shape=(
            shape((rows, depth), BF16),
            shape((rows, width), BF16),
            shape((rows, width), BF16),
            shape((rows, width), BF16),
            shape((depth, E), F32),
            shape((depth, E), F32),
        ),
        in_specs=[ANY] * 7 + [VMEM] * 6,
        out_specs=(VMEM,) * 6,
        scratch_shapes=[
            pltpu.VMEM(part.shape, BF16),
            pltpu.VMEM((7 * rows, depth // 8), BF16),
            pltpu.VMEM(dkv.shape, BF16),
            pltpu.VMEM((15 * rows, dkv.shape[1] // 16), BF16),
            pltpu.VMEM((8 * rows, 2 * E), BF16),
            pltpu.VMEM((depth, 2 * E), BF16),
            pltpu.VMEM((15 * depth // 16, 2 * E), BF16),
            pltpu.VMEM((depth, 2 * E), BF16),
            pltpu.VMEM(states.shape, BF16),
            pltpu.VMEM(residual.shape, BF16),
            pltpu.VMEM(slices.shape, BF16),
            pltpu.VMEM(mid_t.shape, BF16),
            pltpu.VMEM(w_ret.shape, BF16),
            pltpu.VMEM(states.shape, BF16),
            pltpu.SemaphoreType.DMA((7,)),
            *wires(180),
        ],
        compiler_params=params(number),
    )(part, residual, dkv, slices, mid_t, w_ret, states, rq, rk, rv, logs, decays, first_state)


def contract_last(left, right):
    return lax.dot_general(
        left, right, (((1,), (1,)), ((), ())), preferred_element_type=jnp.float32
    )


def local(
    mid,
    second_in,
    cotangent,
    w_key,
    w_value,
    w_query,
    w_out,
    w_ret_out,
    ret_query,
    ret_key,
    ret_value,
    gate,
    decay_exp,
    mask_start,
):
    rate = jnp.exp2(-decay_exp.astype(F32) / 64.0)
    logs = jnp.pad(-rate[:, None] * gate, ((0, 8 - gate.shape[0]), (0, 0)))
    kv, q1, g1, q0, mid_t, slices, first_state, state, decay = open_stage(
        mid, second_in, cotangent, w_key, w_value, w_query, w_out, ret_key, ret_value, logs, 0
    )
    upper_grad, upper_kv = attend(q1, g1, kv, mask_start, None, False)
    upper_in = contract_last(upper_grad, w_query[1])
    upstream, states, decays = upstream_of(upper_in.astype(BF16), cotangent, state, decay, 1)
    g0 = contract_last(upstream, w_out[0]).astype(BF16)
    lower_grad, kv_part = attend(q0, g0, kv, mask_start, upper_kv, True)
    lower_in = contract_last(lower_grad, w_query[0])
    return close_stage(
        lower_in.astype(BF16),
        upstream,
        kv_part,
        slices,
        mid_t,
        w_ret_out,
        states,
        ret_query,
        ret_key,
        ret_value,
        logs,
        decays,
        first_state,
        2,
    )


def solution(mesh):
    torus = Mesh(mesh.devices.reshape(2, 4, 2, 4, 2), ("xh", "y", "core", "z", "xl"))
    in_specs = (
        P(SEQ, None),
        P(SEQ, None),
        P(SEQ, None),
        P(None, HEAD),
        P(None, HEAD),
        P(None, None, HEAD),
        P(None, HEAD, None),
        P(HEAD, None),
        P(SEQ, HEAD),
        P(SEQ, HEAD),
        P(SEQ, HEAD),
        P(HEAD, SEQ),
        P(HEAD),
        P(SEQ),
    )
    out_specs = (
        P(SEQ, None),
        P(SEQ, HEAD),
        P(SEQ, HEAD),
        P(SEQ, HEAD),
        P(None, HEAD),
        P(None, HEAD),
    )
    return jax.shard_map(local, mesh=torus, in_specs=in_specs, out_specs=out_specs, check_vma=False)
```

profile of v0, /device:TPU:1, one launch (start us, length us, event | category | flops | bytes accessed | tf_op | source)
XLA Modules:
  0.0 208.4 jit_solution(18043596326067325095)
XLA Ops:
  0.6 0.7 exponential_negate_fusion
  1.3 0.8 broadcast_multiply_fusion
  2.1 0.6 pad.4.logs
  2.7 32.7 %shard_map.181 = (bf16[4096,256]{1,0:T(8,128)(2,1)}, bf16[256,384]{1,0:T(8,128)(2,1)}, bf16[256,384]{1,0:T(8,128)(2,1)}, bf16[256,384]{1,0:T(8,128)(2,1)}, bf16[...) custom-call(bf16[256,3072]{1,0:T(8,128)(2,1)} %mid_in.1, ...), custom_call_target="tpu_custom_call" | custom-call | tf_op jit(solution)/shard_map/pallas_call | solution.py:680
  35.3 19.0 %shard_map.182 = (bf16[256,384]{1,0:T(8,128)(2,1)}, f32[256,4096]{1,0:T(8,128)}) custom-call(s32[2]{0:T(128)} %refs_0_.3, bf16[256,384]{1,0:T(8,128)(2,1)} %get-tuple-element.23.refs_1_, bf16[256,384]{1,0:T(8,128)(2,1)} %get-tuple-element.24.refs_2_, bf16[4096,256]{1,0:T(8,128)(2,1)} %get-tuple-element.25.refs_3_), custom_call_target="tpu_custom_call" | custom-call | tf_op jit(solution)/shard_map/pallas_call | solution.py:507
  54.3 3.9 %convolution_convert_fusion.1.part = bf16[256,3072]{1,0:T(8,128)(2,1)} fusion(bf16[256,384]{1,0:T(8,128)(2,1)} %get-tuple-element.26, bf16[2,3072,384]{2,1,0:T(8,128)(2,1)} %wq_in.1), kind=kOutput, calls=%fused_computation.1 | convolution fusion | flops 604766208 | bytes 4128768 | tf_op jit(solution)/shard_map/dot_general | solution.py:918
  58.2 0.0 slice-start
  58.2 40.5 %shard_map.183 = (bf16[256,3072]{1,0:T(8,128)(2,1)}, bf16[6144,128]{1,0:T(8,128)(2,1)}, f32[256,128]{1,0:T(8,128)}) custom-call(bf16[256,3072]{1,0:T(8,128)(2,1)} %convolution_convert_fusion.1.part, bf16[256,3072]{1,0:T(8,128)(2,1)} %residual.1, bf16[384,128]{1,0:T(8,128)(2,1)} %get-tuple-element.27.state, f32[16,128]{1,0:T(8,128)} %get-tuple-element.28.decay), custom_call_target="tpu_custom_call" | custom-call | tf_op jit(solution)/shard_map/pallas_call | solution.py:387
  98.8 0.0 slice-start.1
  98.8 4.0 %fusion.7.refs_2_ = bf16[256,384]{1,0:T(8,128)(2,1)} fusion(bf16[256,3072]{1,0:T(8,128)(2,1)} %get-tuple-element.29.res_in, bf16[2,384,3072]{2,1,0:T(8,128)(2,1)} %wo_in.1), kind=kOutput, calls=%fused_computation.9 | convolution fusion | flops 604078080 | bytes 4128768 | tf_op jit(solution)/shard_map/dot_general | solution.py:918
  102.7 19.6 %shard_map.184 = (bf16[256,384]{1,0:T(8,128)(2,1)}, bf16[256,4096]{1,0:T(8,128)(2,1)}) custom-call(s32[2]{0:T(128)} %refs_0_.3, bf16[256,384]{1,0:T(8,128)(2,1)} %get-tuple-element.22.refs_1_, bf16[256,384]{1,0:T(8,128)(2,1)} %fusion.7.refs_2_, bf16[4096,256]{1,0:T(8,128)(2,1)} %get-tuple-element.25.refs_3_, f32[256,4096]{1,0:T(8,128)} %get-tuple-element.30.refs_4_), custom_call_target="tpu_custom_call" | custom-call | tf_op jit(solution)/shard_map/pallas_call | solution.py:507
  122.3 0.0 slice-done
  122.3 0.0 slice-done.1
  122.3 3.1 %convolution_convert_fusion.part_in = bf16[256,3072]{1,0:T(8,128)(2,1)} fusion(bf16[256,384]{1,0:T(8,128)(2,1)} %get-tuple-element.31, bf16[2,3072,384]{2,1,0:T(8,128)(2,1)S(1)} %bitcast.15), kind=kOutput, calls=%fused_computation | convolution fusion | flops 604766208 | bytes 4128768 | tf_op jit(solution)/shard_map/dot_general | solution.py:918
  125.4 75.8 %shard_map.185 = (bf16[256,3072]{1,0:T(8,128)(2,1)}, bf16[256,384]{1,0:T(8,128)(2,1)}, bf16[256,384]{1,0:T(8,128)(2,1)}, bf16[256,384]{1,0:T(8,128)(2,1)}, f32[3072,128]{1,0:T(8,128)}, /*index=5*/f32[3072,128]{1,0:T(8,128)}) custom-call(bf16[256,3072]{1,0:T(8,128)(2,1)} %convolution_convert_fusion.part_in, bf16[256,3072]{1,0:T(8,128)(2,1)} %get-tuple-element.29.res_in, ...), custom_call_target="tpu_custom_call" | custom-call | tf_op jit(solution)/shard_map/pallas_call | solution.py:883
  201.2 0.0 copy-start.4
  201.2 0.0 copy-start.3
  201.2 0.0 copy-start.2
  201.3 0.0 copy-start.1
  201.3 2.8 %copy.26 = bf16[256,3072]{1,0:T(8,128)(2,1)} copy(bf16[256,3072]{1,0:T(8,128)(2,1)} %get-tuple-element.44) | data formatting | bytes 3145728
  204.1 0.0 copy-done.4
  204.1 0.0 copy-start
  204.1 0.7 copy.27
  204.7 0.0 copy-done.3
  204.7 0.7 copy.28
  205.4 0.0 copy-done.2
  205.4 0.7 copy.29
  206.1 0.0 copy-done.1
  206.1 1.1 copy.30
  207.3 0.0 copy-done
  207.3 1.1 copy.31
  (1 shorter events, 0.0 us)
Async XLA Ops:
  58.2 64.1 %slice-start = ((s8[4718592]{0:T(1024)(128)(4,1)}), s8[524288]{0:T(1024)(128)(4,1)S(1)}, s32[]{:S(2)}) async-start(s8[4718592]{0:T(1024)(128)(4,1)} %bitcast.14), calls=%async_computation | async-start | bytes 1048576
  98.8 23.6 %slice-start.1 = ((s8[4718592]{0:T(1024)(128)(4,1)}), s8[4194304]{0:T(1024)(128)(4,1)S(1)}, s32[]{:S(2)}) async-start(s8[4718592]{0:T(1024)(128)(4,1)} %bitcast.14), calls=%async_computation.1 | async-start | bytes 8388608
  201.2 2.8 %copy-start.4 = (bf16[256,384]{1,0:T(8,128)(2,1)S(1)}, bf16[256,384]{1,0:T(8,128)(2,1)}, u32[]{:S(2)}) copy-start(bf16[256,384]{1,0:T(8,128)(2,1)} %get-tuple-element.45) | copy-start | bytes 589828
  201.2 3.5 %copy-start.3 = (bf16[256,384]{1,0:T(8,128)(2,1)S(1)}, bf16[256,384]{1,0:T(8,128)(2,1)}, u32[]{:S(2)}) copy-start(bf16[256,384]{1,0:T(8,128)(2,1)} %get-tuple-element.46) | copy-start | bytes 589828
  201.2 4.2 %copy-start.2 = (bf16[256,384]{1,0:T(8,128)(2,1)S(1)}, bf16[256,384]{1,0:T(8,128)(2,1)}, u32[]{:S(2)}) copy-start(bf16[256,384]{1,0:T(8,128)(2,1)} %get-tuple-element.47) | copy-start | bytes 589828
  201.3 4.9 %copy-start.1 = (f32[3072,128]{1,0:T(8,128)S(1)}, f32[3072,128]{1,0:T(8,128)}, u32[]{:S(2)}) copy-start(f32[3072,128]{1,0:T(8,128)} %get-tuple-element.48) | copy-start | bytes 4718596
  204.1 3.2 %copy-start = (f32[3072,128]{1,0:T(8,128)S(1)}, f32[3072,128]{1,0:T(8,128)}, u32[]{:S(2)}) copy-start(f32[3072,128]{1,0:T(8,128)} %get-tuple-element.49) | copy-start | bytes 4718596
where the time goes:
time: 209 us; the launch traced here: 208 us
  Pallas kernels  188 us (90%)
  matrix products  11 us (5%)
  local copies, waits for them, and re-layouts  7.75 us (4%)
    pallas_call x1, Pallas kernels, close_stage(): pl.pallas_call(close_kernel, out_shape=(shape((rows, depth), BF16), shape...  75.8 us
    pallas_call x1, Pallas kernels, upstream_of(): pl.pallas_call(upstream_kernel, out_shape=(jax.ShapeDtypeStruct(part.shap...  40.5 us
    pallas_call x2, Pallas kernels, attend(): pl.pallas_call(kernel, out_shape=(jax.ShapeDtypeStruct((rows, width), BF1...  38.5 us
    pallas_call x1, Pallas kernels, open_stage(): pl.pallas_call(open_kernel, out_shape=(shape((16 * rows, 2 * E), BF16), s...  32.7 us
    dot_general x3, matrix products, contract_last(): lax.dot_general(left, right, (((1,), (1,)), ((), ())), preferred_element_...  11 us
    unnamed x20, local copies, waits for them, and re-layouts  7.15 us

commit v1 on v0

--- a/solution.py
+++ b/solution.py
@@ -23,6 +23,12 @@
 class Wire:
     def __init__(self, send, recv):
         self.send, self.recv, self.sent, self.used = send, recv, [], 0
+        self.work, self.pace = [], 1
+
+    def idle(self, count):
+        for item in self.work[:count]:
+            item()
+        self.work = self.work[count:]
 
     def put(self, src, dst, to):
         k = self.used
@@ -40,6 +46,7 @@
         return (k, to)
 
     def got(self, ticket, landed):
+        self.idle(self.pace)
         k, to = ticket
         pltpu.make_async_remote_copy(
             src_ref=landed,
@@ -359,50 +366,6 @@
     yield from gather_head(wire, by_columns(out, width), rows)
 
 
-def upstream_kernel(
-    part, residual, state, decay, out, states, decays, acc, land, local, send, recv
-):
-    s_rows, d_rows = state.shape[0], decay.shape[0]
-    s_at, d_at = by_rows(states, s_rows), by_rows(decays, d_rows)
-    me = seq_index()
-    copies = bring(
-        (part, acc), (state, s_at(me, 0, s_rows)), (decay, d_at(me, 0, d_rows)), sem=local
-    )
-    meet(seq_peers() + head_peers())
-    for copy in copies:
-        copy.wait()
-    wire = Wire(send, recv)
-    finish(
-        together(
-            head_run(wire, acc, land, residual, out),
-            gather_seq(wire, s_at, s_rows),
-            gather_seq(wire, d_at, d_rows),
-        )
-    )
-    wire.drain()
-
-
-def upstream_of(part, residual, state, decay, number):
-    rows, columns = part.shape
-    return pl.pallas_call(
-        upstream_kernel,
-        out_shape=(
-            jax.ShapeDtypeStruct(part.shape, BF16),
-            jax.ShapeDtypeStruct((16 * state.shape[0], state.shape[1]), BF16),
-            jax.ShapeDtypeStruct((16 * decay.shape[0], decay.shape[1]), F32),
-        ),
-        in_specs=[ANY, VMEM, ANY, ANY],
-        out_specs=(VMEM, VMEM, VMEM),
-        scratch_shapes=[
-            pltpu.VMEM(part.shape, BF16),
-            pltpu.VMEM((7 * rows, columns // 8), BF16),
-            pltpu.SemaphoreType.DMA((3,)),
-            *wires(90),
-        ],
-        compiler_params=params(number),
-    )(part, residual, state, decay)
-
-
 def dot_last(a, b):
     return lax.dot_general(a, b, (((1,), (1,)), ((), ())), preferred_element_type=F32)
 
@@ -429,108 +392,6 @@
         column = lax.broadcasted_iota(jnp.int32, (rows, CHUNK), 1) + k
         seen = (column >= low) & (column <= high)
         bias[:, k : k + CHUNK] = jnp.where(seen, 0.0, -jnp.inf)
-
-
-def one_head(q, g, kv, bias, raised, rounded, total, first):
-    length = kv.shape[0]
-    rows = q.shape[0]
-    factor = 1.0 / math.sqrt(E)
-    chunks = [slice(k, k + CHUNK) for k in range(0, length, CHUNK)]
-    top = None
-    for k in chunks:
-        scores = dot_last(q, kv[k, :E]) + bias[:, k]
-        raised[:, k] = scores
-        most = folded(scores, jnp.maximum)
-        top = most if top is None else jnp.maximum(top, most)
-    top = jnp.max(top, axis=1, keepdims=True)
-    whole = None
-    for k in chunks:
-        power = jnp.exp2((raised[:, k] - top) * (factor * math.log2(math.e)))
-        raised[:, k] = power
-        part = folded(power, jnp.add)
-        whole = part if whole is None else whole + part
-    inverse = 1.0 / jnp.sum(whole, axis=1, keepdims=True)
-    outputs = jnp.zeros((rows, E), F32)
-    for k in chunks:
-        near_probs = (raised[:, k] * inverse).astype(BF16)
-        rounded[:, k] = near_probs
-        outputs = outputs + dot(near_probs, kv[k, E:])
-    outputs = outputs.astype(BF16).astype(F32)
-    delta = jnp.sum(g.astype(F32) * outputs, axis=1, keepdims=True)
-    scaled = inverse * factor
-    q_t = q.astype(F32).T.astype(BF16)
-    g_t = g.astype(F32).T.astype(BF16)
-    query_grad = jnp.zeros((rows, E), F32)
-    for k in chunks:
-        dprobs = dot_last(g, kv[k, E:])
-        dscores = ((raised[:, k] * scaled) * (dprobs - delta)).astype(BF16)
-        query_grad = query_grad + dot(dscores, kv[k, :E])
-        total[:E, k] = total[:E, k] + dot(q_t, dscores)
-        total[E:, k] = total[E:, k] + dot(g_t, rounded[:, k])
-    return query_grad.astype(BF16)
-
-
-def attend_kernel(firsts, q, g, kv, before, q_grad, after, bias, raised, rounded):
-    rows, length = q.shape[0], kv.shape[0]
-    fill_bias(bias, firsts, seq_index() * rows, rows, length)
-    if before is None:
-        after[...] = jnp.zeros_like(after)
-    else:
-        after[...] = before[...]
-
-    def head(h, _):
-        at = pl.ds(pl.multiple_of(h * E, E), E)
-        q_grad[:, at] = one_head(q[:, at], g[:, at], kv, bias, raised, rounded, after, h)
-        return 0
-
-    lax.fori_loop(0, q.shape[1] // E, head, 0)
-
-
-def attend(queries, grad_out, kv, firsts, before, final):
-    rows, width = queries.shape
-    length = kv.shape[0]
-    kept = BF16 if final else F32
-    operands = [firsts, queries, grad_out, kv]
-    specs = [pl.BlockSpec(memory_space=pltpu.SMEM), VMEM, VMEM, VMEM]
-    if before is not None:
-        operands.append(before)
-        specs.append(VMEM)
-
-    def kernel(*refs):
-        ins, rest = list(refs[: len(operands)]), refs[len(operands) :]
-        if before is None:
-            ins.append(None)
-        q_grad, after, total, bias, raised, rounded = rest
-        attend_kernel(*ins, q_grad, total, bias, raised, rounded)
-        after[...] = total[...].astype(kept)
-
-    return pl.pallas_call(
-        kernel,
-        out_shape=(
-            jax.ShapeDtypeStruct((rows, width), BF16),
-            jax.ShapeDtypeStruct((2 * E, length), kept),
-        ),
-        in_specs=specs,
-        out_specs=(VMEM, VMEM),
-        scratch_shapes=[
-            pltpu.VMEM((2 * E, length), F32),
-            pltpu.VMEM((rows, length), F32),
-            pltpu.VMEM((rows, length), F32),
-            pltpu.VMEM((rows, length), BF16),
-        ],
-        compiler_params=pltpu.CompilerParams(vmem_limit_bytes=56 * 1024 * 1024),
-    )(*operands)
-
-
-def weave(run, work, steps):
-    work = list(work)
-    each = -(-len(work) // steps)
-    for _ in run:
-        for item in work[:each]:
-            item()
-        work = work[each:]
-    for item in work:
-        item()
 
 
 def flipped(value):
@@ -566,8 +427,8 @@
 
 
 def open_kernel(
-    mid_in, second_in, cot_in, wk_in, wv_in, wq_in, wo_in, ret_key, ret_value, logs,
-    kv, q1, g1, q0, mid_t, slices, first_state, state, decay,
+    mid_in, second_in, cot_in, wk_in, wv_in, wq_in, wo_in, ret_key, ret_value, gate, decay_exp,
+    kv, q1, g1, q0, mid_t, slices, first_state, state, decay, logs,
     mid, second, cot, wkv, wq1, wo1, wq0, flip, kept, local, sent, send, recv,
 ):
     rows = mid.shape[0]
@@ -577,17 +438,20 @@
         (mid_in, mid),
         (wk_in, wkv.at[:, pl.ds(0, E)]),
         (wv_in, wkv.at[:, pl.ds(E, E)]),
+        sem=local,
+    )
+    places = spread(7)
+    meet(seq_peers() + [{"z": a, "xl": b} for (a, b), _ in places])
+    for copy in copies:
+        copy.wait()
+    copies += bring(
         (second_in, second),
         (wq_in.at[1], wq1),
         (cot_in, cot),
         (wo_in.at[1], wo1),
         (wq_in.at[0], wq0),
-        sem=local,
-    )
-    places = spread(7)
-    meet(seq_peers() + [{"z": a, "xl": b} for (a, b), _ in places])
-    for copy in copies[:3]:
-        copy.wait()
+        sem=local.at[pl.ds(3, 5)],
+    )
     wire = Wire(send, recv)
     at = by_rows(kv, rows)
     at(seq_index(), 0, rows)[...] = dot(mid[...], wkv[...]).astype(BF16)
@@ -612,16 +476,17 @@
     work = []
 
     def product(out, left, right, how, number):
-        def first():
-            copies[number].wait()
-            if number != 7:
-                copies[number - 1].wait()
-            out[:, : 2 * E] = how(left, right, 0, 2 * E).astype(BF16)
-
-        def rest():
-            out[:, 2 * E :] = how(left, right, 2 * E, E).astype(BF16)
-
-        work.extend((first, rest))
+        def part(k):
+            def go():
+                if k == 0:
+                    copies[number].wait()
+                    if number != 7:
+                        copies[number - 1].wait()
+                out[:, k : k + E] = how(left, right, k, E).astype(BF16)
+
+            return go
+
+        work.extend(part(k) for k in range(0, out.shape[1], E))
 
     def straight(left, right, at, count):
         return dot(left[...], right[:, at : at + count])
@@ -629,9 +494,15 @@
     def across(left, right, at, count):
         return dot_last(left[...], right[at : at + count])
 
-    product(q1, second, wq1, straight, 4)
-    product(g1, cot, wo1, across, 6)
-    product(q0, mid, wq0, straight, 7)
+    def rates():
+        row = lax.broadcasted_iota(jnp.int32, (8, 128), 0)
+        rate = jnp.zeros((8, 128), F32)
+        for r in range(gate.shape[0]):
+            power = jnp.full((8, 128), decay_exp[r], jnp.int32).astype(F32)
+            rate = jnp.where(row == r, jnp.exp2(power * (-1.0 / 64.0)), rate)
+        empty = jnp.zeros((8 - gate.shape[0], gate.shape[1]), F32)
+        tall = jnp.concatenate((gate[...], empty), axis=0)
+        logs[...] = -rate[:, :1] * tall
 
     def states():
         arow, acol = log_decays(logs[...])
@@ -650,8 +521,6 @@
             last = jnp.exp(arow[1][r : r + 1, RC - 1 :])
             state[cols] = (last * made[0] + made[1]).astype(BF16)
 
-    work.append(states)
-
     def turn(k):
         def go():
             for j in range(k, k + 512, 128):
@@ -659,8 +528,13 @@
 
         return go
 
-    work.extend(turn(k) for k in range(0, mid.shape[1], 512))
-    weave(together(gather_seq(wire, at, rows), exchange()), work, 6)
+    product(q1, second, wq1, straight, 4)
+    product(g1, cot, wo1, across, 6)
+    product(q0, mid, wq0, straight, 7)
+    turns = [turn(k) for k in range(0, mid.shape[1], 512)]
+    wire.work = [rates, states, turns[0]] + work + turns[1:]
+    finish(together(gather_seq(wire, at, rows), exchange()))
+    wire.idle(len(wire.work))
     own.wait()
     outs = [
         pltpu.make_async_copy(flip, mid_t, sent.at[1]),
@@ -673,7 +547,8 @@
         copy.wait()
 
 
-def open_stage(mid, second_in, cot, w_key, w_value, w_query, w_out, ret_key, ret_value, logs, number):
+def open_stage(number, *operands):
+    mid, w_query = operands[0], operands[5]
     rows, depth = mid.shape
     wide = w_query.shape[2]
     shape = jax.ShapeDtypeStruct
@@ -689,9 +564,10 @@
             shape((wide, E), F32),
             shape((wide, E), BF16),
             shape((16, 128), F32),
+            shape((8, rows), F32),
         ),
-        in_specs=[ANY] * 7 + [VMEM] * 3,
-        out_specs=(VMEM, VMEM, VMEM, VMEM, ANY, ANY, VMEM, VMEM, VMEM),
+        in_specs=[ANY] * 7 + [VMEM] * 3 + [pl.BlockSpec(memory_space=pltpu.SMEM)],
+        out_specs=(VMEM, VMEM, VMEM, VMEM, ANY, ANY, VMEM, VMEM, VMEM, VMEM),
         scratch_shapes=[
             pltpu.VMEM((rows, depth), BF16),
             pltpu.VMEM((rows, depth), BF16),
@@ -707,15 +583,15 @@
             *wires(30),
         ],
         compiler_params=params(number),
-    )(mid, second_in, cot, w_key, w_value, w_query, w_out, ret_key, ret_value, logs)
+    )(*operands)
 
 
 def close_kernel(
-    part_in, res_in, dkv_in, slices_in, mid_t_in, w_ret_in, states_in,
-    rq, rk, rv, logs, decays, first_state,
-    grad_mid, gq, gk, gv, gwk, gwv,
-    acc_m, land_m, acc_k, land_k, kv_all, w_acc, w_land, w_sum, grads,
-    residual, slices, mid_t, w_ret, states, local, send, recv,
+    part_in, dkv_in, slices_in, mid_t_in, w_ret_in, states_in,
+    own_res, rq, rk, rv, logs, decays, first_state,
+    mid_out, gq, gk, gv, w_sum,
+    grad_mid, acc_m, land_m, acc_k, land_k, kv_all, w_acc, w_land, grads,
+    slices, mid_t, w_ret, states, local, send, recv,
 ):
     rows, depth = acc_m.shape
     share = depth // 8
@@ -726,7 +602,6 @@
         (part_in, acc_m),
         (mid_t_in, mid_t),
         (slices_in, slices),
-        (res_in, residual),
         (w_ret_in, w_ret),
         (states_in, states),
         sem=local,
@@ -771,7 +646,7 @@
         entering[r, 1] = (jnp.exp(end(r, 0)) * now + first_state[cols]).astype(BF16)
 
     def early():
-        copies[6].wait()
+        copies[5].wait()
 
     work = [early]
     for r in range(heads):
@@ -787,7 +662,9 @@
         kv_at(me, 0, rows)[...] = total.T.astype(BF16)
 
     m_at = by_columns(acc_m, share)
-    weave(together(keys(), scatter_head(wire, m_at, rows, land_m)), work, 3)
+    wire.work = work
+    finish(together(keys(), scatter_head(wire, m_at, rows, land_m)))
+    wire.idle(len(wire.work))
     own_kv = kv_at(me, 0, rows)
     gather_kv = gather_head(wire, kv_at, rows)
     next(gather_kv)
@@ -807,9 +684,7 @@
     next(shared)
     finish(gather_kv)
     copies[3].wait()
-    copies[4].wait()
-    total = m_at(me, 0, rows)[...].astype(F32)
-    total = total + residual[:, pl.ds(pl.multiple_of(me * share, 128), share)].astype(F32)
+    total = m_at(me, 0, rows)[...].astype(F32) + own_res[...].astype(F32)
     for h in range(8):
         total = total + dot_last(kv_at(h, 0, rows)[...], slices[h])
     out_at = by_columns(grad_mid, share)
@@ -820,7 +695,9 @@
             next(shared, None)
 
     beside(gather_head(wire, out_at, rows))
-    copies[5].wait()
+    shown = pltpu.make_async_copy(grad_mid, mid_out, local.at[6])
+    shown.start()
+    copies[4].wait()
     grad_o = dot_last(grad_mid[...], w_ret[...]).astype(BF16)
     own_grad = {}
     for r, c in pieces:
@@ -845,14 +722,9 @@
             dot(second[r, c], g) * (1.0 / E),
         )
 
-    work = [lambda r=r, c=c: inside(r, c) for r, c in pieces]
-
-    def both():
-        for _ in back:
-            next(shared, None)
-            yield
-
-    weave(both(), work, 5)
+    wire.work = [lambda r=r, c=c: inside(r, c) for r, c in pieces]
+    beside(back)
+    wire.idle(len(wire.work))
     for r in range(heads):
         now = jnp.zeros((E, E), F32)
         for k in range(15, 0, -1):
@@ -869,16 +741,14 @@
         ).astype(BF16)
         gv[span, cols] = (inner[r, c][1] + shrink * dot(rk[span, cols], after[r, c])).astype(BF16)
     finish(shared)
-    gwk[...] = w_sum[:, :E].astype(F32)
-    gwv[...] = w_sum[:, E:].astype(F32)
+    shown.wait()
     wire.drain()
 
 
-def close_stage(
-    part, residual, dkv, slices, mid_t, w_ret, states, rq, rk, rv, logs, decays, first_state, number
-):
+def close_stage(number, *operands):
+    part, dkv, slices, mid_t, w_ret, states = operands[:6]
     rows, depth = part.shape
-    width = rq.shape[1]
+    width = operands[7].shape[1]
     shape = jax.ShapeDtypeStruct
     return pl.pallas_call(
         close_kernel,
@@ -887,12 +757,12 @@
             shape((rows, width), BF16),
             shape((rows, width), BF16),
             shape((rows, width), BF16),
-            shape((depth, E), F32),
-            shape((depth, E), F32),
+            shape((depth, 2 * E), BF16),
         ),
-        in_specs=[ANY] * 7 + [VMEM] * 6,
-        out_specs=(VMEM,) * 6,
+        in_specs=[ANY] * 6 + [VMEM] * 7,
+        out_specs=(ANY, VMEM, VMEM, VMEM, VMEM),
         scratch_shapes=[
+            pltpu.VMEM(part.shape, BF16),
             pltpu.VMEM(part.shape, BF16),
             pltpu.VMEM((7 * rows, depth // 8), BF16),
             pltpu.VMEM(dkv.shape, BF16),
@@ -900,9 +770,7 @@
             pltpu.VMEM((8 * rows, 2 * E), BF16),
             pltpu.VMEM((depth, 2 * E), BF16),
             pltpu.VMEM((15 * depth // 16, 2 * E), BF16),
-            pltpu.VMEM((depth, 2 * E), BF16),
             pltpu.VMEM(states.shape, BF16),
-            pltpu.VMEM(residual.shape, BF16),
             pltpu.VMEM(slices.shape, BF16),
             pltpu.VMEM(mid_t.shape, BF16),
             pltpu.VMEM(w_ret.shape, BF16),
@@ -911,13 +779,249 @@
             *wires(180),
         ],
         compiler_params=params(number),
-    )(part, residual, dkv, slices, mid_t, w_ret, states, rq, rk, rv, logs, decays, first_state)
-
-
-def contract_last(left, right):
-    return lax.dot_general(
-        left, right, (((1,), (1,)), ((), ())), preferred_element_type=jnp.float32
-    )
+    )(*operands)
+
+
+def hand_out_kernel(*refs):
+    ins, outs, held, (wide, sem_in, sem_out) = refs[:5], refs[5:11], refs[11:16], refs[16:]
+    copies = bring(*zip(ins, held), sem=sem_in)
+    sends = []
+    for k in range(4):
+        copies[k].wait()
+        sends.append(pltpu.make_async_copy(held[k], outs[k], sem_out.at[k]))
+        sends[-1].start()
+    copies[4].wait()
+    for k in range(2):
+        wide[k] = held[4][:, k * E : (k + 1) * E].astype(F32)
+        sends.append(pltpu.make_async_copy(wide.at[k], outs[4 + k], sem_out.at[4 + k]))
+        sends[-1].start()
+    for send in sends:
+        send.wait()
+
+
+def hand_out(*arrays):
+    shape = jax.ShapeDtypeStruct
+    depth = arrays[4].shape[0]
+    return pl.pallas_call(
+        hand_out_kernel,
+        out_shape=tuple(shape(a.shape, a.dtype) for a in arrays[:4])
+        + (shape((depth, E), F32), shape((depth, E), F32)),
+        in_specs=[ANY] * 5,
+        out_specs=(ANY,) * 6,
+        scratch_shapes=[pltpu.VMEM(a.shape, a.dtype) for a in arrays]
+        + [
+            pltpu.VMEM((2, depth, E), F32),
+            pltpu.SemaphoreType.DMA((5,)),
+            pltpu.SemaphoreType.DMA((6,)),
+        ],
+    )(*arrays)
+
+
+def scores_pass(q, kv, bias, raised, stats):
+    def part(k):
+        def go():
+            for at in (slice(k, k + CHUNK), slice(k + CHUNK, k + 2 * CHUNK)):
+                scores = dot_last(q(), kv[at, :E]) + bias[:, at]
+                raised[:, at] = scores
+                most = folded(scores, jnp.maximum)
+                top = stats.get("top")
+                stats["top"] = most if top is None else jnp.maximum(top, most)
+
+        return go
+
+    return [part(k) for k in range(0, kv.shape[0], 2 * CHUNK)]
+
+
+def power_pass(raised, stats):
+    def part(k):
+        def go():
+            if k == 0:
+                stats["top"] = jnp.max(stats["top"], axis=1, keepdims=True)
+            for at in (slice(k, k + CHUNK), slice(k + CHUNK, k + 2 * CHUNK)):
+                shifted = raised[:, at] - stats["top"]
+                power = jnp.exp2(shifted * (math.log2(math.e) / math.sqrt(E)))
+                raised[:, at] = power
+                more = folded(power, jnp.add)
+                stats["sum"] = stats["sum"] + more if "sum" in stats else more
+
+        return go
+
+    return [part(k) for k in range(0, raised.shape[1], 2 * CHUNK)]
+
+
+def output_pass(kv, raised, rounded, inverse, outputs, stats):
+    def part(k):
+        def go():
+            if k == 0:
+                whole = jnp.sum(stats["sum"], axis=1, keepdims=True)
+                stats["inverse"] = 1.0 / whole
+                inverse[...] = jnp.broadcast_to(stats["inverse"], inverse.shape)
+            for at in (slice(k, k + CHUNK), slice(k + CHUNK, k + 2 * CHUNK)):
+                probs = (raised[:, at] * stats["inverse"]).astype(BF16)
+                rounded[:, at] = probs
+                made = dot(probs, kv[at, E:])
+                stats["out"] = stats["out"] + made if "out" in stats else made
+            if k + 2 * CHUNK == kv.shape[0]:
+                outputs(stats["out"].astype(BF16))
+
+        return go
+
+    return [part(k) for k in range(0, kv.shape[0], 2 * CHUNK)]
+
+
+def forward_parts(q, kv, bias, raised, rounded, inverse, outputs):
+    stats = {}
+    return (
+        scores_pass(q, kv, bias, raised, stats)
+        + power_pass(raised, stats)
+        + output_pass(kv, raised, rounded, inverse, outputs, stats)
+    )
+
+
+def backward(q, g, kv, raised, rounded, inverse, outputs, total):
+    length = kv.shape[0]
+    delta = jnp.sum(g.astype(F32) * outputs.astype(F32), axis=1, keepdims=True)
+    scaled = inverse[:, :1] * (1.0 / math.sqrt(E))
+    q_t = flipped(q).astype(BF16)
+    g_t = flipped(g).astype(BF16)
+    query_grad = jnp.zeros(q.shape, F32)
+    for k in range(0, length, CHUNK):
+        at = slice(k, k + CHUNK)
+        dprobs = dot_last(g, kv[at, E:])
+        dscores = ((raised[:, at] * scaled) * (dprobs - delta)).astype(BF16)
+        query_grad = query_grad + dot(dscores, kv[at, :E])
+        total[:E, at] = total[:E, at] + dot(q_t, dscores)
+        total[E:, at] = total[E:, at] + dot(g_t, rounded[:, at])
+    return query_grad.astype(BF16)
+
+
+def middle_kernel(
+    wq_in, wo_in, cot_in, state, decay, firsts, q1, g1, q0, kv,
+    part, dkv, own_up, states, decays,
+    bias, total, raised, rounded, inverse, outputs, q_grad, g0,
+    wq1, wq0, wo0, residual, upstream, acc, land, local, send, recv,
+):
+    rows, depth = acc.shape
+    length = kv.shape[0]
+    share = depth // 8
+    heads = q1.shape[1] // E
+    s_rows, d_rows = state.shape[0], decay.shape[0]
+    s_at, d_at = by_rows(states, s_rows), by_rows(decays, d_rows)
+    me, here = head_index(), seq_index()
+    copies = bring(
+        (wq_in.at[1], wq1),
+        (cot_in, residual),
+        (state, s_at(here, 0, s_rows)),
+        (decay, d_at(here, 0, d_rows)),
+        (wo_in.at[0], wo0),
+        (wq_in.at[0], wq0),
+        sem=local,
+    )
+    fill_bias(bias, firsts, here * rows, rows, length)
+    total[...] = jnp.zeros_like(total)
+
+    def keep(cols):
+        def put(value):
+            outputs[:, cols] = value
+
+        return put
+
+    def back(h, g):
+        cols = pl.ds(pl.multiple_of(h * E, E), E)
+        return cols, lambda q: backward(
+            q[:, cols], g[:, cols], kv, raised.at[h], rounded.at[h], inverse.at[h],
+            outputs[:, cols], total,
+        )
+
+    def upper(h, _):
+        cols, run = back(h, g1)
+        for item in forward_parts(
+            lambda: q1[:, cols], kv, bias, raised.at[h], rounded.at[h], inverse.at[h], keep(cols)
+        ):
+            item()
+        q_grad[:, cols] = run(q1)
+        return 0
+
+    lax.fori_loop(0, heads, upper, 0)
+    copies[0].wait()
+    for k in range(0, depth, share):
+        acc[:, k : k + share] = dot_last(q_grad[...], wq1[k : k + share]).astype(BF16)
+    meet(seq_peers() + head_peers())
+    for copy in copies[1:4]:
+        copy.wait()
+    wire = Wire(send, recv)
+    for h in range(heads):
+        cols = slice(h * E, (h + 1) * E)
+        wire.work += forward_parts(
+            lambda cols=cols: q0[:, cols],
+            kv, bias, raised.at[h], rounded.at[h], inverse.at[h], keep(cols),
+        )
+    finish(
+        together(
+            head_run(wire, acc, land, residual, upstream),
+            gather_seq(wire, s_at, s_rows),
+            gather_seq(wire, d_at, d_rows),
+        )
+    )
+    wire.idle(len(wire.work))
+    copies[4].wait()
+    g0[...] = dot_last(upstream[...], wo0[...]).astype(BF16)
+
+    def lower(h, _):
+        cols, run = back(h, g0)
+        q_grad[:, cols] = run(q0)
+        return 0
+
+    lax.fori_loop(0, heads, lower, 0)
+    dkv[...] = total[...].astype(BF16)
+    copies[5].wait()
+    for k in range(0, depth, share):
+        part[:, k : k + share] = dot_last(q_grad[...], wq0[k : k + share]).astype(BF16)
+    own_up[...] = by_columns(upstream, share)(me, 0, rows)[...]
+    wire.drain()
+
+
+def middle_stage(number, *operands):
+    w_query, w_out, cot, state, decay = operands[:5]
+    q1, kv = operands[6], operands[9]
+    rows, depth = cot.shape
+    wide, length = q1.shape[1], kv.shape[0]
+    heads = wide // E
+    shape = jax.ShapeDtypeStruct
+    return pl.pallas_call(
+        middle_kernel,
+        out_shape=(
+            shape((rows, depth), BF16),
+            shape((2 * E, length), BF16),
+            shape((rows, depth // 8), BF16),
+            shape((16 * state.shape[0], E), BF16),
+            shape((16 * decay.shape[0], 128), F32),
+        ),
+        in_specs=[ANY] * 5 + [pl.BlockSpec(memory_space=pltpu.SMEM)] + [VMEM] * 4,
+        out_specs=(VMEM,) * 5,
+        scratch_shapes=[
+            pltpu.VMEM((rows, length), F32),
+            pltpu.VMEM((2 * E, length), F32),
+            pltpu.VMEM((heads, rows, length), F32),
+            pltpu.VMEM((heads, rows, length), BF16),
+            pltpu.VMEM((heads, rows, 128), F32),
+            pltpu.VMEM((rows, wide), BF16),
+            pltpu.VMEM((rows, wide), BF16),
+            pltpu.VMEM((rows, wide), BF16),
+            pltpu.VMEM((depth, wide), BF16),
+            pltpu.VMEM((depth, wide), BF16),
+            pltpu.VMEM((wide, depth), BF16),
+            pltpu.VMEM((rows, depth), BF16),
+            pltpu.VMEM((rows, depth), BF16),
+            pltpu.VMEM((rows, depth), BF16),
+            pltpu.VMEM((7 * rows, depth // 8), BF16),
+            pltpu.SemaphoreType.DMA((6,)),
+            *wires(90),
+        ],
+        compiler_params=pltpu.CompilerParams(
+            collective_id=number, has_side_effects=True, vmem_limit_bytes=67043328
+        ),
+    )(*operands)
 
 
 def local(
@@ -936,33 +1040,18 @@
     decay_exp,
     mask_start,
 ):
-    rate = jnp.exp2(-decay_exp.astype(F32) / 64.0)
-    logs = jnp.pad(-rate[:, None] * gate, ((0, 8 - gate.shape[0]), (0, 0)))
-    kv, q1, g1, q0, mid_t, slices, first_state, state, decay = open_stage(
-        mid, second_in, cotangent, w_key, w_value, w_query, w_out, ret_key, ret_value, logs, 0
-    )
-    upper_grad, upper_kv = attend(q1, g1, kv, mask_start, None, False)
-    upper_in = contract_last(upper_grad, w_query[1])
-    upstream, states, decays = upstream_of(upper_in.astype(BF16), cotangent, state, decay, 1)
-    g0 = contract_last(upstream, w_out[0]).astype(BF16)
-    lower_grad, kv_part = attend(q0, g0, kv, mask_start, upper_kv, True)
-    lower_in = contract_last(lower_grad, w_query[0])
-    return close_stage(
-        lower_in.astype(BF16),
-        upstream,
-        kv_part,
-        slices,
-        mid_t,
-        w_ret_out,
-        states,
-        ret_query,
-        ret_key,
-        ret_value,
-        logs,
-        decays,
-        first_state,
-        2,
-    )
+    kv, q1, g1, q0, mid_t, slices, first_state, state, decay, logs = open_stage(
+        0, mid, second_in, cotangent, w_key, w_value, w_query, w_out, ret_key, ret_value, gate,
+        decay_exp,
+    )
+    part, dkv, own_up, states, decays = middle_stage(
+        1, w_query, w_out, cotangent, state, decay, mask_start, q1, g1, q0, kv
+    )
+    made = close_stage(
+        2, part, dkv, slices, mid_t, w_ret_out, states, own_up, ret_query, ret_key, ret_value,
+        logs, decays, first_state,
+    )
+    return hand_out(*made)
 
 
 def solution(mesh):

time: 209 us -> 184 us (0.88)
  matrix products: 11 us -> 0 us
  local copies, waits for them, and re-layouts: 7.75 us -> 0 us
  Pallas kernels: 188 us -> 183 us
    dot_general x3 -> x0, matrix products: 11 us -> none  [contract_last(): lax.dot_general(left, right, (((1,), (1,)), ((), ())), preferred_element_...]
    unnamed x20 -> x0, local copies, waits for them, and re-layouts: 7.15 us -> none
    pallas_call x3 -> x2, Pallas kernels: 79 us -> 72.3 us  [the longest x1 68.3 us: middle_stage(): pl.pallas_call(middle_kernel, out_shape=(shape((rows, depth), BF16), shap...]
where the time goes in v1:
time: 184 us; the launch traced here: 183 us
  Pallas kernels  183 us (99%)
    pallas_call x1, Pallas kernels, close_stage(): pl.pallas_call(close_kernel, out_shape=(shape((rows, depth), BF16), shape...  77.3 us
    pallas_call x1, Pallas kernels, middle_stage(): pl.pallas_call(middle_kernel, out_shape=(shape((rows, depth), BF16), shap...  68.3 us
    pallas_call x1, Pallas kernels, open_stage(): pl.pallas_call(open_kernel, out_shape=(shape((16 * rows, 2 * E), BF16), s...  33 us
    pallas_call x1, Pallas kernels, hand_out(): pl.pallas_call(hand_out_kernel, out_shape=tuple((shape(a.shape, a.dtype)...  3.92 us

profile of v1, /device:TPU:1, one launch (start us, length us, event | category | flops | bytes accessed | tf_op | source)
XLA Modules:
  0.0 183.4 jit_solution(439909196681880800)
XLA Ops:
  0.6 33.0 %shard_map.181 = (bf16[4096,256]{1,0:T(8,128)(2,1)}, bf16[256,384]{1,0:T(8,128)(2,1)}, bf16[256,384]{1,0:T(8,128)(2,1)}, bf16[256,384]{1,0:T(8,128)(2,1)}, bf16[...) custom-call(bf16[256,3072]{1,0:T(8,128)(2,1)} %mid_in.1, ...), custom_call_target="tpu_custom_call" | custom-call | tf_op jit(solution)/shard_map/pallas_call | solution.py:555
  33.7 68.3 %shard_map.182 = (bf16[256,3072]{1,0:T(8,128)(2,1)}, bf16[256,4096]{1,0:T(8,128)(2,1)}, bf16[256,384]{1,0:T(8,128)(2,1)}, bf16[6144,128]{1,0:T(8,128)(2,1)}, f32[256,128]{1,0:T(8,128)}) custom-call(bf16[2,3072,384]{2,1,0:T(8,128)(2,1)} %wq_in.3, bf16[2,384,3072]{2,1,0:T(8,128)(2,1)} %wo_in.3, bf16[256,3072]{1,0:T(8,128)(2,1)} %cot_in.3, ...), custom_call_target="tpu_custom_call" | custom-call | tf_op jit(solution)/shard_map/pallas_call | solution.py:991
  102.0 77.3 %shard_map.183 = (bf16[256,3072]{1,0:T(8,128)(2,1)}, bf16[256,384]{1,0:T(8,128)(2,1)}, bf16[256,384]{1,0:T(8,128)(2,1)}, bf16[256,384]{1,0:T(8,128)(2,1)}, bf16[3072,256]{1,0:T(8,128)(2,1)}) custom-call(bf16[256,3072]{1,0:T(8,128)(2,1)} %get-tuple-element.32.part_in, bf16[256,4096]{1,0:T(8,128)(2,1)} %get-tuple-element.33.dkv_in, ...), custom_call_target="tpu_custom_call" | custom-call | tf_op jit(solution)/shard_map/pallas_call | solution.py:753
  179.3 3.9 %shard_map.184 = (bf16[256,3072]{1,0:T(8,128)(2,1)}, bf16[256,384]{1,0:T(8,128)(2,1)}, bf16[256,384]{1,0:T(8,128)(2,1)}, bf16[256,384]{1,0:T(8,128)(2,1)}, f32[3072,128]{1,0:T(8,128)}, /*index=5*/f32[3072,128]{1,0:T(8,128)}) custom-call(bf16[256,3072]{1,0:T(8,128)(2,1)} %get-tuple-element.41.refs_0_, bf16[256,384]{1,0:T(8,128)(2,1)} %get-tuple-element.42.refs_1_, ...), custom_call_target="tpu_custom_call" | custom-call | tf_op jit(solution)/shard_map/pallas_call | solution.py:805

commit v2 on v1

v2 whole, which is shorter than its diff:
```python
import functools
import math

import jax
import jax.numpy as jnp
from jax import lax
from jax.experimental import pallas as pl
from jax.experimental.pallas import tpu as pltpu
from jax.sharding import Mesh
from jax.sharding import PartitionSpec as P

E = 128
BLK = 128
RC = 128
SEQ = ("xh", "y", "core")
HEAD = ("z", "xl")

MESH = pl.DeviceIdType.MESH
BF16 = jnp.bfloat16
F32 = jnp.float32


class Wire:
    def __init__(self, send, recv):
        self.send, self.recv, self.sent, self.used = send, recv, [], 0
        self.work, self.pace = [], 1

    def idle(self, count):
        for item in self.work[:count]:
            item()
        self.work = self.work[count:]

    def put(self, src, dst, to):
        k = self.used
        self.used += 1
        copy = pltpu.make_async_remote_copy(
            src_ref=src,
            dst_ref=dst,
            send_sem=self.send.at[k],
            recv_sem=self.recv.at[k],
            device_id=to,
            device_id_type=MESH,
        )
        copy.start()
        self.sent.append(copy)
        return (k, to)

    def got(self, ticket, landed):
        self.idle(self.pace)
        k, to = ticket
        pltpu.make_async_remote_copy(
            src_ref=landed,
            dst_ref=landed,
            send_sem=self.send.at[k],
            recv_sem=self.recv.at[k],
            device_id=to,
            device_id_type=MESH,
        ).wait_recv()

    def drain(self):
        for copy in self.sent:
            copy.wait_send()
        self.sent = []


def greet(peers):
    barrier = pltpu.get_barrier_semaphore()
    for to in peers:
        pl.semaphore_signal(barrier, inc=1, device_id=to, device_id_type=MESH)


def answered(peers):
    pl.semaphore_wait(pltpu.get_barrier_semaphore(), len(peers))


def near(axis):
    at = lax.axis_index(axis)
    return at, lax.rem(at + 1, 4), lax.rem(at + 3, 4), lax.rem(at + 2, 4)


def seq_peers():
    y, yp, ym, y2 = near("y")
    return [
        {"xh": 1 - lax.axis_index("xh")},
        {"y": yp},
        {"y": ym},
        {"core": 1 - lax.axis_index("core")},
    ]


def head_peers():
    z, zp, zm, z2 = near("z")
    return [{"xl": 1 - lax.axis_index("xl")}, {"z": zp}, {"z": zm}]


def by_rows(ref, rows, parts=2):
    step = rows // parts

    def at(slot, first, count):
        return ref.at[pl.ds(pl.multiple_of(slot * rows + first, step), count)]

    return at


def by_columns(ref, width):
    def at(slot, first, count):
        return ref.at[pl.ds(first, count), pl.ds(pl.multiple_of(slot * width, 128), width)]

    return at


def add_to(total, part):
    total[...] = (total[...].astype(F32) + part[...].astype(F32)).astype(total.dtype)


def together(*runs):
    runs = list(runs)
    while runs:
        for run in list(runs):
            try:
                next(run)
            except StopIteration:
                runs.remove(run)
        yield


def finish(run):
    for _ in run:
        pass


def gather_seq(wire, at, rows):
    xh, c = lax.axis_index("xh"), lax.axis_index("core")
    y, yp, ym, y2 = near("y")
    xo, co = 1 - xh, 1 - c
    half = rows // 2
    whole, low, high = (0, rows), (0, half), (half, half)
    across, up, down, beside = {"xh": xo}, {"y": yp}, {"y": ym}, {"core": co}

    def slot(a, b, d):
        return a * 8 + b * 2 + d

    def pass_on(s, part, to):
        return wire.put(at(s, *part), at(s, *part), to)

    side = []
    own, far = slot(xh, y, c), slot(xo, y, c)
    t_x = pass_on(own, whole, across)
    ups, downs = [pass_on(own, whole, up)], [pass_on(own, whole, down)]
    side.append((pass_on(own, whole, beside), slot(xh, y, co)))
    yield
    wire.got(t_x, at(far, *whole))
    ups.append(pass_on(far, whole, up))
    downs.append(pass_on(far, whole, down))
    side.append((pass_on(far, whole, beside), slot(xo, y, co)))
    yield
    last = []
    for k, q in enumerate((xh, xo)):
        wire.got(ups[k], at(slot(q, ym, c), *whole))
        a = pass_on(slot(q, ym, c), low, up)
        side.append((pass_on(slot(q, ym, c), whole, beside), slot(q, ym, co)))
        wire.got(downs[k], at(slot(q, yp, c), *whole))
        b = pass_on(slot(q, yp, c), high, down)
        side.append((pass_on(slot(q, yp, c), whole, beside), slot(q, yp, co)))
        last.append((a, b))
        yield
    for k, q in enumerate((xh, xo)):
        wire.got(last[k][0], at(slot(q, y2, c), *low))
        wire.got(last[k][1], at(slot(q, y2, c), *high))
        side.append((pass_on(slot(q, y2, c), whole, beside), slot(q, y2, co)))
        yield
    for ticket, s in side:
        wire.got(ticket, at(s, *whole))


def ring_scatter(wire, at, slot, axis, first, count, land, before=None):
    r, rp, rm, r2 = near(axis)
    up, down = {axis: rp}, {axis: rm}
    half = count // 2
    wait = before or (lambda j: None)
    low, high = land.at[pl.ds(0, half)], land.at[pl.ds(half, half)]
    from_up, from_down = land.at[pl.ds(count, count)], land.at[pl.ds(2 * count, count)]
    wait(2)
    a = wire.put(at(slot(r2), first, half), low, up)
    b = wire.put(at(slot(r2), first + half, half), high, down)
    yield
    wait(1)
    wire.got(a, low)
    add_to(at(slot(rp), first, half), low)
    u = wire.put(at(slot(rp), first, count), from_down, up)
    wait(3)
    wire.got(b, high)
    add_to(at(slot(rm), first + half, half), high)
    d = wire.put(at(slot(rm), first, count), from_up, down)
    yield
    wait(0)
    wire.got(u, from_down)
    add_to(at(slot(r), first, count), from_down)
    wire.got(d, from_up)
    add_to(at(slot(r), first, count), from_up)


def scatter_seq(wire, at, rows, land):
    xh, c = lax.axis_index("xh"), lax.axis_index("core")
    y, yp, ym, y2 = near("y")
    xo, co = 1 - xh, 1 - c

    def slot(a, b, d):
        return a * 8 + b * 2 + d

    def block(k, count=1):
        return land.at[pl.ds(k * rows, count * rows)]

    places = {0: y, 1: yp, 2: y2, 3: ym}
    side = {}
    for n, q in enumerate((xo, xh)):
        for m, j in enumerate((2, 1, 3, 0)):
            dst = block(4 * n + m)
            side[n, j] = (wire.put(at(slot(q, places[j], co), 0, rows), dst, {"core": co}), dst)

    def before(n, q):
        def wait(j):
            ticket, dst = side[n, j]
            wire.got(ticket, dst)
            add_to(at(slot(q, places[j], c), 0, rows), dst)

        return wait

    def ring(n, q):
        return ring_scatter(
            wire, at, lambda j: slot(q, j, c), "y", 0, rows, block(8 + 3 * n, 3), before(n, q)
        )

    sent = []

    def far():
        yield from ring(0, xo)
        sent.append(wire.put(at(slot(xo, y, c), 0, rows), block(14), {"xh": xo}))

    yield from together(far(), ring(1, xh))
    wire.got(sent[0], block(14))
    return block(14)


def scatter_head(wire, at, rows, land):
    xl = lax.axis_index("xl")
    z, zp, zm, z2 = near("z")
    xo = 1 - xl
    half = rows // 2

    def slot(j, q):
        return j * 2 + q

    def block(k, count=1):
        return land.at[pl.ds(k * half, count * half)]

    places = {0: z, 1: zp, 2: z2, 3: zm}
    side = {}
    for m, j in enumerate((2, 1, 3, 0)):
        side[j] = (wire.put(at(slot(places[j], xo), 0, half), block(m), {"xl": xo}), block(m))

    def wait(j):
        ticket, dst = side[j]
        wire.got(ticket, dst)
        add_to(at(slot(places[j], xl), 0, half), dst)

    sent = []

    def far():
        yield from ring_scatter(
            wire, at, lambda j: slot(j, xo), "z", half, half, block(4, 3)
        )
        sent.append(wire.put(at(slot(z, xo), half, half), block(13), {"xl": xo}))

    yield from together(
        far(),
        ring_scatter(wire, at, lambda j: slot(j, xl), "z", half, half, block(7, 3)),
        ring_scatter(wire, at, lambda j: slot(j, xl), "z", 0, half, block(10, 3), wait),
    )
    wire.got(sent[0], block(13))
    add_to(at(slot(z, xl), half, half), block(13))


def gather_head(wire, at, rows):
    xl = lax.axis_index("xl")
    z, zp, zm, z2 = near("z")
    xo = 1 - xl
    half = rows // 2
    up, down, across = {"z": zp}, {"z": zm}, {"xl": xo}

    def slot(j, q):
        return j * 2 + q

    def pass_on(s, first, count, to):
        return wire.put(at(s, first, count), at(s, first, count), to)

    def ring(q, first, each=None):
        h = half // 2
        tell = each or (lambda j: None)
        a = pass_on(slot(z, q), first, half, up)
        b = pass_on(slot(z, q), first, half, down)
        tell(z)
        yield
        wire.got(a, at(slot(zm, q), first, half))
        c = pass_on(slot(zm, q), first, h, up)
        tell(zm)
        wire.got(b, at(slot(zp, q), first, half))
        d = pass_on(slot(zp, q), first + h, h, down)
        tell(zp)
        yield
        wire.got(c, at(slot(z2, q), first, h))
        wire.got(d, at(slot(z2, q), first + h, h))
        tell(z2)

    side = []

    def tell(j):
        side.append((pass_on(slot(j, xl), 0, half, across), slot(j, xo)))

    t_x = pass_on(slot(z, xl), half, half, across)

    def far():
        wire.got(t_x, at(slot(z, xo), half, half))
        yield from ring(xo, half)

    yield from together(ring(xl, 0, tell), ring(xl, half), far())
    for ticket, s in side:
        wire.got(ticket, at(s, 0, half))


ANY = pl.BlockSpec(memory_space=pl.ANY)
VMEM = pl.BlockSpec(memory_space=pltpu.VMEM)


def bring(*pairs, sem):
    copies = [pltpu.make_async_copy(s, d, sem.at[k]) for k, (s, d) in enumerate(pairs)]
    for copy in copies:
        copy.start()
    return copies


def seq_index():
    return lax.axis_index("xh") * 8 + lax.axis_index("y") * 2 + lax.axis_index("core")


def head_index():
    return lax.axis_index("z") * 2 + lax.axis_index("xl")


def total_into(out_at, acc_at, residual, rows, width):
    me = head_index()
    own = acc_at(me, 0, rows)
    kept = residual.at[pl.ds(0, rows), pl.ds(pl.multiple_of(me * width, 128), width)]
    out_at(me, 0, rows)[...] = (kept[...].astype(F32) + own[...].astype(F32)).astype(BF16)


def head_run(wire, acc, land, residual, out):
    rows, columns = acc.shape
    width = columns // 8
    yield from scatter_head(wire, by_columns(acc, width), rows, land)
    total_into(by_columns(out, width), by_columns(acc, width), residual, rows, width)
    yield from gather_head(wire, by_columns(out, width), rows)


def dot_last(a, b):
    return lax.dot_general(a, b, (((1,), (1,)), ((), ())), preferred_element_type=F32)


def dot(a, b):
    return jnp.dot(a, b, preferred_element_type=F32)


def folded(value, op):
    parts = [value[:, k : k + 128] for k in range(0, value.shape[1], 128)]
    while len(parts) > 1:
        parts = [op(a, b) for a, b in zip(parts[::2], parts[1::2])]
    return parts[0]


CHUNK = 512


def fill_bias(bias, firsts, position, rows, length):
    row = lax.broadcasted_iota(jnp.int32, (rows, CHUNK), 0)
    low = jnp.where(row < BLK, firsts[0], firsts[1])
    high = row + position
    for k in range(0, length, CHUNK):
        column = lax.broadcasted_iota(jnp.int32, (rows, CHUNK), 1) + k
        seen = (column >= low) & (column <= high)
        bias[:, k : k + CHUNK] = jnp.where(seen, 0.0, -jnp.inf)


def flipped(value):
    return value.astype(F32).T


def log_decays(logs):
    t = lax.broadcasted_iota(jnp.int32, (RC, RC), 0)
    s = lax.broadcasted_iota(jnp.int32, (RC, RC), 1)
    upto = jnp.where(t <= s, 1.0, 0.0)
    rows, columns = [], []
    for c in range(logs.shape[1] // RC):
        part = jnp.dot(
            logs[:, c * RC : (c + 1) * RC],
            upto,
            precision=lax.Precision.HIGHEST,
            preferred_element_type=F32,
        )
        rows.append(part)
        tall = jnp.concatenate((part, jnp.zeros((RC - part.shape[0], RC), F32)), axis=0)
        columns.append(tall.T)
    return rows, columns


def spread(peers):
    z, xl = lax.axis_index("z"), lax.axis_index("xl")
    places = []
    for k in range(1, 8):
        to = (lax.rem(z + k // 2, 4), lax.rem(xl + k, 2))
        came = (lax.rem(z + 4 - k // 2, 4), lax.rem(xl + k, 2))
        places.append((to, came))
    return places


def hand_out_kernel(*refs):
    ins, outs, held, (wide, sem_in, sem_out) = refs[:5], refs[5:11], refs[11:16], refs[16:]
    copies = bring(*zip(ins, held), sem=sem_in)
    sends = []
    for k in range(4):
        copies[k].wait()
        sends.append(pltpu.make_async_copy(held[k], outs[k], sem_out.at[k]))
        sends[-1].start()
    copies[4].wait()
    for k in range(2):
        wide[k] = held[4][:, k * E : (k + 1) * E].astype(F32)
        sends.append(pltpu.make_async_copy(wide.at[k], outs[4 + k], sem_out.at[4 + k]))
        sends[-1].start()
    for send in sends:
        send.wait()


def hand_out(*arrays):
    shape = jax.ShapeDtypeStruct
    depth = arrays[4].shape[0]
    return pl.pallas_call(
        hand_out_kernel,
        out_shape=tuple(shape(a.shape, a.dtype) for a in arrays[:4])
        + (shape((depth, E), F32), shape((depth, E), F32)),
        in_specs=[ANY] * 5,
        out_specs=(ANY,) * 6,
        scratch_shapes=[pltpu.VMEM(a.shape, a.dtype) for a in arrays]
        + [
            pltpu.VMEM((2, depth, E), F32),
            pltpu.SemaphoreType.DMA((5,)),
            pltpu.SemaphoreType.DMA((6,)),
        ],
    )(*arrays)


def scores_pass(q, kv, bias, raised, stats):
    def part(k):
        def go():
            for at in (slice(k, k + CHUNK), slice(k + CHUNK, k + 2 * CHUNK)):
                scores = dot_last(q(), kv[at, :E]) + bias[:, at]
                raised[:, at] = scores
                most = folded(scores, jnp.maximum)
                top = stats.get("top")
                stats["top"] = most if top is None else jnp.maximum(top, most)

        return go

    return [part(k) for k in range(0, kv.shape[0], 2 * CHUNK)]


def power_pass(raised, stats):
    def part(k):
        def go():
            if k == 0:
                stats["top"] = jnp.max(stats["top"], axis=1, keepdims=True)
            for at in (slice(k, k + CHUNK), slice(k + CHUNK, k + 2 * CHUNK)):
                shifted = raised[:, at] - stats["top"]
                power = jnp.exp2(shifted * (math.log2(math.e) / math.sqrt(E)))
                raised[:, at] = power
                more = folded(power, jnp.add)
                stats["sum"] = stats["sum"] + more if "sum" in stats else more

        return go

    return [part(k) for k in range(0, raised.shape[1], 2 * CHUNK)]


def output_pass(kv, raised, rounded, inverse, outputs, stats):
    def part(k):
        def go():
            if k == 0:
                whole = jnp.sum(stats["sum"], axis=1, keepdims=True)
                stats["inverse"] = 1.0 / whole
                inverse[...] = jnp.broadcast_to(stats["inverse"], inverse.shape)
            for at in (slice(k, k + CHUNK), slice(k + CHUNK, k + 2 * CHUNK)):
                probs = (raised[:, at] * stats["inverse"]).astype(BF16)
                rounded[:, at] = probs
                made = dot(probs, kv[at, E:])
                stats["out"] = stats["out"] + made if "out" in stats else made
            if k + 2 * CHUNK == kv.shape[0]:
                outputs(stats["out"].astype(BF16))

        return go

    return [part(k) for k in range(0, kv.shape[0], 2 * CHUNK)]


def forward_parts(q, kv, bias, raised, rounded, inverse, outputs):
    stats = {}
    return (
        scores_pass(q, kv, bias, raised, stats)
        + power_pass(raised, stats)
        + output_pass(kv, raised, rounded, inverse, outputs, stats)
    )


def backward(q, g, kv, raised, rounded, inverse, outputs, total):
    length = kv.shape[0]
    delta = jnp.sum(g.astype(F32) * outputs.astype(F32), axis=1, keepdims=True)
    scaled = inverse[:, :1] * (1.0 / math.sqrt(E))
    q_t = flipped(q).astype(BF16)
    g_t = flipped(g).astype(BF16)
    query_grad = jnp.zeros(q.shape, F32)
    for k in range(0, length, CHUNK):
        at = slice(k, k + CHUNK)
        dprobs = dot_last(g, kv[at, E:])
        dscores = ((raised[:, at] * scaled) * (dprobs - delta)).astype(BF16)
        query_grad = query_grad + dot(dscores, kv[at, :E])
        total[:E, at] = total[:E, at] + dot(q_t, dscores)
        total[E:, at] = total[E:, at] + dot(g_t, rounded[:, at])
    return query_grad.astype(BF16)


def opening(r, wire, copies, work):
    rows, depth = r.mid.shape

    def product(out, left, right, how, *numbers):
        def part(k):
            def go():
                if k == 0:
                    for number in numbers:
                        copies[number].wait()
                out[:, k : k + E] = how(left, right, k, E).astype(BF16)

            return go

        work.extend(part(k) for k in range(0, out.shape[1], E))

    def straight(left, right, at, count):
        return dot(left[...], right[:, at : at + count])

    def across(left, right, at, count):
        return dot_last(left[...], right[at : at + count])

    def rates():
        row = lax.broadcasted_iota(jnp.int32, (8, 128), 0)
        rate = jnp.zeros((8, 128), F32)
        for k in range(r.gate.shape[0]):
            power = jnp.full((8, 128), r.decay_exp[k], jnp.int32).astype(F32)
            rate = jnp.where(row == k, jnp.exp2(power * (-1.0 / 64.0)), rate)
        empty = jnp.zeros((8 - r.gate.shape[0], r.gate.shape[1]), F32)
        tall = jnp.concatenate((r.gate[...], empty), axis=0)
        r.logs[...] = -rate[:, :1] * tall

    def states():
        arow, acol = log_decays(r.logs[...])
        total = arow[0][:, RC - 1 :] + arow[1][:, RC - 1 :]
        here = seq_index()
        mine = r.decays.at[pl.ds(pl.multiple_of(here * 16, 16), 16)]
        mine[...] = jnp.concatenate(
            (jnp.broadcast_to(total, (8, 128)), jnp.zeros((8, 128), F32)), axis=0
        )
        count = r.ret_key.shape[1]
        for h in range(count // E):
            cols = slice(h * E, (h + 1) * E)
            made = []
            for c in range(2):
                span = slice(c * RC, (c + 1) * RC)
                shrink = jnp.exp(arow[c][h : h + 1, RC - 1 :] - acol[c][:, h : h + 1])
                scaled = (shrink * r.ret_key[span, cols].astype(F32)).astype(BF16)
                made.append(dot(flipped(scaled).astype(BF16), r.ret_value[span, cols]))
            r.first_state[cols] = made[0]
            last = jnp.exp(arow[1][h : h + 1, RC - 1 :])
            to = r.states.at[pl.ds(pl.multiple_of(here * count + h * E, E), E)]
            to[...] = (last * made[0] + made[1]).astype(BF16)

    def turn(k):
        def go():
            for j in range(k, k + 512, 128):
                r.mid_t[j : j + 128] = flipped(r.mid[:, j : j + 128]).astype(BF16)

        return go

    turns = [turn(k) for k in range(0, depth, 512)]
    work.extend([rates, states, turns[0]])
    product(r.q1, r.second, r.wq1, straight, 3, 4)
    product(r.g1, r.residual, r.wo, across, 5, 6)
    product(r.q0, r.mid, r.wq0, straight, 7)
    work.extend(turns[1:])


def exchange(r, wire, places):
    me, c = head_index(), lax.axis_index("core")
    share = r.wkv.shape[0] // 8
    tickets, side = [], []

    def mine(slot, half):
        return r.slices.at[slot, :, pl.ds(pl.multiple_of(half * E, E), E)]

    for (a, b), (ca, cb) in places:
        rows = pl.ds(pl.multiple_of((a * 2 + b) * share, share), share)
        src = r.wkv.at[rows, pl.ds(pl.multiple_of(c * E, E), E)]
        tickets.append((wire.put(src, mine(me, c), {"z": a, "xl": b}), ca * 2 + cb))
    yield
    for ticket, slot in tickets:
        wire.got(ticket, mine(slot, c))
        side.append((wire.put(mine(slot, c), mine(slot, c), {"core": 1 - c}), slot))
        yield
    for ticket, slot in side:
        wire.got(ticket, mine(slot, 1 - c))


def closing(r, wire, run_states):
    rows, depth = r.acc.shape
    share = depth // 8
    heads = r.ret_query.shape[1] // E
    me, here = head_index(), seq_index()
    kv_at = by_rows(r.kv_all, rows, 4)
    w_rows = depth // 16
    w_at = by_rows(r.w_sum, w_rows)
    s_rows = heads * E
    s_at = by_rows(r.grads, s_rows)
    arow, acol = log_decays(r.logs[...])
    t = lax.broadcasted_iota(jnp.int32, (RC, RC), 0)
    s = lax.broadcasted_iota(jnp.int32, (RC, RC), 1)
    pieces = [(h, c) for h in range(heads) for c in range(2)]
    where = {(h, c): (slice(c * RC, (c + 1) * RC), slice(h * E, (h + 1) * E)) for h, c in pieces}
    weights, second, turned, entering, after = {}, {}, {}, {}, {}
    rq, rk, rv = r.ret_query, r.ret_key, r.ret_value

    def end(h, c):
        return arow[c][h : h + 1, RC - 1 :]

    def prepare(h, c):
        a_t, a_s = acol[c][:, h : h + 1], arow[c][h : h + 1]
        lower = t >= s
        weights[h, c] = jnp.where(lower, jnp.exp(jnp.where(lower, a_t - a_s, 0.0)), 0.0)
        q, k = rq[where[h, c]], rk[where[h, c]]
        both = (weights[h, c] * dot_last(q, k)).astype(BF16)
        second[h, c] = flipped(both).astype(BF16)
        grown = (jnp.exp(a_t) * q.astype(F32)).astype(BF16)
        turned[h, c] = flipped(grown).astype(BF16)

    def arriving(h):
        cols = where[h, 0][1]
        now = jnp.zeros((E, E), F32)
        for k in range(15):
            mine = r.states[k * s_rows + h * E : k * s_rows + (h + 1) * E].astype(F32)
            new = jnp.exp(r.decays[k * 16 + h : k * 16 + h + 1]) * now + mine
            now = jnp.where(k < here, new, now)
        entering[h, 0] = now.astype(BF16)
        entering[h, 1] = (jnp.exp(end(h, 0)) * now + r.first_state[cols]).astype(BF16)

    def keys():
        at = by_columns(r.acc_k, rows)
        rest = yield from scatter_seq(wire, at, rows, r.land_k)
        own = at(here, 0, rows)
        total = own[...].astype(F32) + rest[...].astype(F32)
        kv_at(me, 0, rows)[...] = total.T.astype(BF16)

    run_keys = keys()
    next(run_keys)
    for k in range(0, depth, share):
        r.acc[:, k : k + share] = dot_last(r.q_grad[...], r.wq0[k : k + share]).astype(BF16)
    wire.work = [lambda h=h: arriving(h) for h in range(heads)]
    wire.work += [lambda h=h, c=c: prepare(h, c) for h, c in pieces]
    m_at = by_columns(r.acc, share)
    finish(together(scatter_head(wire, m_at, rows, r.land), run_keys))
    wire.idle(len(wire.work))
    own_kv = kv_at(me, 0, rows)
    gather_kv = gather_head(wire, kv_at, rows)
    next(gather_kv)
    r.wkv[...] = dot(r.mid_t[...], own_kv[...]).astype(BF16)

    def sums():
        at = by_rows(r.wkv, w_rows)
        rest = yield from scatter_seq(wire, at, w_rows, r.w_land)
        w_at(here, 0, w_rows)[...] = (
            at(here, 0, w_rows)[...].astype(F32) + rest[...].astype(F32)
        ).astype(BF16)
        yield
        yield from gather_seq(wire, w_at, w_rows)

    shared = sums()
    next(shared)

    def beside(run):
        for _ in run:
            next(shared, None)

    beside(gather_kv)
    total = m_at(me, 0, rows)[...].astype(F32)
    total = total + by_columns(r.upstream, share)(me, 0, rows)[...].astype(F32)
    for h in range(8):
        total = total + dot_last(kv_at(h, 0, rows)[...], r.slices[h])
    out_at = by_columns(r.mid, share)
    out_at(me, 0, rows)[...] = total.astype(BF16)
    beside(gather_head(wire, out_at, rows))
    shown = [pltpu.make_async_copy(r.mid, r.grad_mid, r.local.at[0])]
    shown[0].start()
    grad_o = dot_last(r.mid[...], r.wo[...]).astype(BF16)
    own_grad = {}
    for h, c in pieces:
        span, cols = where[h, c]
        own_grad[h, c] = dot(turned[h, c], grad_o[span, cols]) * (1.0 / E)
    for h in range(heads):
        made = own_grad[h, 0] + jnp.exp(end(h, 0)) * own_grad[h, 1]
        r.grads[pl.ds(pl.multiple_of(here * s_rows + h * E, E), E)] = made.astype(BF16)
    back = gather_seq(wire, s_at, s_rows)
    next(back)
    inner = {}

    def inside(h, c):
        span, cols = where[h, c]
        g, q, k, v = grad_o[span, cols], rq[span, cols], rk[span, cols], rv[span, cols]
        first = (weights[h, c] * dot_last(g, v)).astype(BF16)
        grow = jnp.exp(acol[c][:, h : h + 1])
        carried = grow * dot_last(g, entering[h, c])
        r.gq[span, cols] = ((dot(first, k) + carried) * (1.0 / E)).astype(BF16)
        inner[h, c] = (
            dot(flipped(first).astype(BF16), q) * (1.0 / E),
            dot(second[h, c], g) * (1.0 / E),
        )

    wire.work = [lambda h=h, c=c: inside(h, c) for h, c in pieces]
    beside(back)
    wire.idle(len(wire.work))
    for h in range(heads):
        now = jnp.zeros((E, E), F32)
        for k in range(15, 0, -1):
            mine = r.grads[k * s_rows + h * E : k * s_rows + (h + 1) * E].astype(F32)
            new = mine + jnp.exp(r.decays[k * 16 + h : k * 16 + h + 1]) * now
            now = jnp.where(k > here, new, now)
        after[h, 1] = now.astype(BF16)
        after[h, 0] = (own_grad[h, 1] + jnp.exp(end(h, 1)) * now).astype(BF16)
    for h, c in pieces:
        span, cols = where[h, c]
        shrink = jnp.exp(end(h, c) - acol[c][:, h : h + 1])
        r.gk[span, cols] = (
            inner[h, c][0] + shrink * dot_last(rv[span, cols], after[h, c])
        ).astype(BF16)
        r.gv[span, cols] = (inner[h, c][1] + shrink * dot(rk[span, cols], after[h, c])).astype(BF16)
    finish(shared)
    for copy in shown:
        copy.wait()
    wire.drain()


class Refs:
    def __init__(self, names, refs):
        for name, ref in zip(names, refs, strict=True):
            setattr(self, name, ref)


IN_NAMES = (
    "mid_in", "second_in", "cot_in", "wk_in", "wv_in", "wq_in", "wo_in", "wr_in",
    "ret_query", "ret_key", "ret_value", "gate", "decay_exp", "firsts",
)
OUT_NAMES = ("grad_mid", "gq", "gk", "gv", "w_sum")


def whole_kernel(names, *refs):
    r = Refs(names, refs)
    rows, depth = r.mid.shape
    length = r.kv.shape[0]
    share = depth // 8
    heads = r.q1.shape[1] // E
    here = seq_index()
    copies = bring(
        (r.mid_in, r.mid),
        (r.wk_in, r.wkv.at[:, pl.ds(0, E)]),
        (r.wv_in, r.wkv.at[:, pl.ds(E, E)]),
        sem=r.local,
    )
    places = spread(7)
    peers = seq_peers() + [{"z": a, "xl": b} for (a, b), _ in places]
    greet(peers)
    for copy in copies:
        copy.wait()
    copies += bring(
        (r.second_in, r.second),
        (r.wq_in.at[1], r.wq1),
        (r.cot_in, r.residual),
        (r.wo_in.at[1], r.wo),
        (r.wq_in.at[0], r.wq0),
        sem=r.local.at[pl.ds(3, 5)],
    )
    wire = Wire(r.send, r.recv)
    at = by_rows(r.kv, rows)
    at(here, 0, rows)[...] = dot(r.mid[...], r.wkv[...]).astype(BF16)
    answered(peers)
    opening(r, wire, copies, wire.work)
    wire.work.append(lambda: fill_bias(r.bias, r.firsts, here * rows, rows, length))

    def clear():
        r.total[...] = jnp.zeros_like(r.total)

    wire.work.append(clear)
    run_kv = gather_seq(wire, at, rows)
    next(run_kv)
    next(run_kv)
    run_slices = exchange(r, wire, places)
    next(run_slices)
    me = head_index()
    own = pltpu.make_async_copy(
        r.wkv.at[pl.ds(pl.multiple_of(me * share, share), share)], r.slices.at[me], r.local.at[8]
    )
    own.start()
    finish(run_kv)
    wire.idle(len(wire.work))
    s_rows = heads * E
    run_states = together(
        gather_seq(wire, by_rows(r.states, s_rows), s_rows),
        gather_seq(wire, by_rows(r.decays, 16), 16),
        run_slices,
    )
    next(run_states)
    late = bring((r.wo_in.at[0], r.wo), sem=r.local.at[pl.ds(9, 1)])

    def keep(cols):
        def put(value):
            r.outputs[:, cols] = value

        return put

    def ahead(h, q, cols):
        return forward_parts(
            lambda: q[:, cols],
            r.kv, r.bias, r.raised.at[h], r.rounded.at[h], r.inverse.at[h], keep(cols),
        )

    def wide(h):
        return pl.ds(pl.multiple_of(h * E, E), E)

    def upper(h, _):
        for item in ahead(h, r.q1, wide(h)):
            item()
        return 0

    def back(q, g):
        def go(h, _):
            cols = wide(h)
            r.q_grad[:, cols] = backward(
                q[:, cols], g[:, cols], r.kv, r.raised.at[h], r.rounded.at[h], r.inverse.at[h],
                r.outputs[:, cols], r.total,
            )
            return 0

        return go

    lax.fori_loop(0, heads, upper, 0)
    next(run_states)
    lax.fori_loop(0, heads, back(r.q1, r.g1), 0)
    next(run_states)
    for k in range(0, depth, share):
        r.acc[:, k : k + share] = dot_last(r.q_grad[...], r.wq1[k : k + share]).astype(BF16)
    for h in range(heads):
        wire.work += ahead(h, r.q0, slice(h * E, (h + 1) * E))
    finish(
        together(
            head_run(wire, r.acc, r.land, r.residual, r.upstream),
            run_states,
        )
    )
    wire.idle(len(wire.work))
    own.wait()
    late[0].wait()
    r.g0[...] = dot_last(r.upstream[...], r.wo[...]).astype(BF16)
    last = bring((r.wr_in, r.wo), sem=r.local.at[pl.ds(10, 1)])
    lax.fori_loop(0, heads, back(r.q0, r.g0), 0)
    r.acc_k[...] = r.total[...].astype(BF16)
    last[0].wait()
    wire.drain()
    closing(r, wire, run_states)


def whole(number, *operands):
    rows, depth = operands[0].shape
    wide = operands[8].shape[1]
    heads = wide // E
    length = 16 * rows
    shape = jax.ShapeDtypeStruct
    scratch = {
        "mid": pltpu.VMEM((rows, depth), BF16),
        "second": pltpu.VMEM((rows, depth), BF16),
        "residual": pltpu.VMEM((rows, depth), BF16),
        "wkv": pltpu.VMEM((depth, 2 * E), BF16),
        "wq1": pltpu.VMEM((depth, wide), BF16),
        "wq0": pltpu.VMEM((depth, wide), BF16),
        "wo": pltpu.VMEM((wide, depth), BF16),
        "mid_t": pltpu.VMEM((depth, rows), BF16),
        "slices": pltpu.VMEM((8, depth // 8, 2 * E), BF16),
        "kv": pltpu.VMEM((length, 2 * E), BF16),
        "q1": pltpu.VMEM((rows, wide), BF16),
        "g1": pltpu.VMEM((rows, wide), BF16),
        "q0": pltpu.VMEM((rows, wide), BF16),
        "outputs": pltpu.VMEM((rows, wide), BF16),
        "logs": pltpu.VMEM((8, rows), F32),
        "first_state": pltpu.VMEM((wide, E), F32),
        "states": pltpu.VMEM((16 * wide, E), BF16),
        "decays": pltpu.VMEM((256, 128), F32),
        "bias": pltpu.VMEM((rows, length), F32),
        "total": pltpu.VMEM((2 * E, length), F32),
        "raised": pltpu.VMEM((heads, rows, length), F32),
        "rounded": pltpu.VMEM((heads, rows, length), BF16),
        "inverse": pltpu.VMEM((heads, rows, 128), F32),
        "upstream": pltpu.VMEM((rows, depth), BF16),
        "land": pltpu.VMEM((7 * rows, depth // 8), BF16),
        "acc_k": pltpu.VMEM((2 * E, length), BF16),
        "land_k": pltpu.VMEM((15 * rows, rows), BF16),
        "kv_all": pltpu.VMEM((8 * rows, 2 * E), BF16),
        "w_land": pltpu.VMEM((15 * depth // 16, 2 * E), BF16),
        "grads": pltpu.VMEM((16 * wide, E), BF16),
        "local": pltpu.SemaphoreType.DMA((11,)),
        "send": pltpu.SemaphoreType.DMA((320,)),
        "recv": pltpu.SemaphoreType.DMA((320,)),
    }
    names = IN_NAMES + OUT_NAMES + tuple(scratch)
    shared = {"acc": "second", "g0": "g1", "q_grad": "gq"}

    def kernel(*refs):
        again = [refs[names.index(name)] for name in shared.values()]
        whole_kernel(names + tuple(shared), *refs, *again)

    smem = pl.BlockSpec(memory_space=pltpu.SMEM)
    return pl.pallas_call(
        kernel,
        out_shape=(
            shape((rows, depth), BF16),
            shape((rows, wide), BF16),
            shape((rows, wide), BF16),
            shape((rows, wide), BF16),
            shape((depth, 2 * E), BF16),
        ),
        in_specs=[ANY] * 8 + [VMEM] * 4 + [smem] * 2,
        out_specs=(ANY, VMEM, VMEM, VMEM, VMEM),
        scratch_shapes=list(scratch.values()),
        compiler_params=pltpu.CompilerParams(
            collective_id=number, has_side_effects=True, vmem_limit_bytes=67043328
        ),
    )(*operands)


def local(
    mid,
    second_in,
    cotangent,
    w_key,
    w_value,
    w_query,
    w_out,
    w_ret_out,
    ret_query,
    ret_key,
    ret_value,
    gate,
    decay_exp,
    mask_start,
):
    made = whole(
        0, mid, second_in, cotangent, w_key, w_value, w_query, w_out, w_ret_out,
        ret_query, ret_key, ret_value, gate, decay_exp, mask_start,
    )
    return hand_out(*made)


def solution(mesh):
    torus = Mesh(mesh.devices.reshape(2, 4, 2, 4, 2), ("xh", "y", "core", "z", "xl"))
    in_specs = (
        P(SEQ, None),
        P(SEQ, None),
        P(SEQ, None),
        P(None, HEAD),
        P(None, HEAD),
        P(None, None, HEAD),
        P(None, HEAD, None),
        P(HEAD, None),
        P(SEQ, HEAD),
        P(SEQ, HEAD),
        P(SEQ, HEAD),
        P(HEAD, SEQ),
        P(HEAD),
        P(SEQ),
    )
    out_specs = (
        P(SEQ, None),
        P(SEQ, HEAD),
        P(SEQ, HEAD),
        P(SEQ, HEAD),
        P(None, HEAD),
        P(None, HEAD),
    )
    return jax.shard_map(local, mesh=torus, in_specs=in_specs, out_specs=out_specs, check_vma=False)
```

time: 184 us -> 158 us (0.86)
  Pallas kernels: 183 us -> 157 us
    pallas_call x3 -> x1, Pallas kernels: 179 us -> 153 us  [whole(): pl.pallas_call(kernel, out_shape=(shape((rows, depth), BF16), shape((rows...]
where the time goes in v2:
time: 158 us
  Pallas kernels  157 us (99%)
    pallas_call x1, Pallas kernels, whole(): pl.pallas_call(kernel, out_shape=(shape((rows, depth), BF16), shape((rows...  153 us
    pallas_call x1, Pallas kernels, hand_out(): pl.pallas_call(hand_out_kernel, out_shape=tuple((shape(a.shape, a.dtype)...  3.92 us

profile of v2, /device:TPU:1, one launch (start us, length us, event | category | flops | bytes accessed | tf_op | source)
XLA Modules:
  0.0 158.2 jit_solution(134340344092233661)
XLA Ops:
  0.6 153.5 %shard_map.181 = (bf16[256,3072]{1,0:T(8,128)(2,1)}, bf16[256,384]{1,0:T(8,128)(2,1)}, bf16[256,384]{1,0:T(8,128)(2,1)}, bf16[256,384]{1,0:T(8,128)(2,1)}, bf16[3072,256]{1,0:T(8,128)(2,1)}) custom-call(bf16[256,3072]{1,0:T(8,128)(2,1)} %refs_0_.1, bf16[256,3072]{1,0:T(8,128)(2,1)} %refs_1_.1, bf16[256,3072]{1,0:T(8,128)(2,1)} %refs_2_.1, ...), custom_call_target="tpu_custom_call" | custom-call | tf_op jit(solution)/shard_map/pallas_call | solution.py:940
  154.1 3.9 %shard_map.182 = (bf16[256,3072]{1,0:T(8,128)(2,1)}, bf16[256,384]{1,0:T(8,128)(2,1)}, bf16[256,384]{1,0:T(8,128)(2,1)}, bf16[256,384]{1,0:T(8,128)(2,1)}, f32[3072,128]{1,0:T(8,128)}, /*index=5*/f32[3072,128]{1,0:T(8,128)}) custom-call(bf16[256,3072]{1,0:T(8,128)(2,1)} %get-tuple-element.11.refs_0_, bf16[256,384]{1,0:T(8,128)(2,1)} %get-tuple-element.12.refs_1_, ...), custom_call_target="tpu_custom_call" | custom-call | tf_op jit(solution)/shard_map/pallas_call | solution.py:445

commit v3 on v2

--- a/solution.py
+++ b/solution.py
@@ -23,7 +23,10 @@
 class Wire:
     def __init__(self, send, recv):
         self.send, self.recv, self.sent, self.used = send, recv, [], 0
-        self.work, self.pace = [], 1
+        self.work, self.pace, self.plan, self.waits = [], 1, {}, 0
+
+    def planned(self, work, plan):
+        self.work, self.pace, self.plan, self.waits = work, 0, plan, 0
 
     def idle(self, count):
         for item in self.work[:count]:
@@ -46,7 +49,8 @@
         return (k, to)
 
     def got(self, ticket, landed):
-        self.idle(self.pace)
+        self.idle(self.plan.get(self.waits, self.pace))
+        self.waits += 1
         k, to = ticket
         pltpu.make_async_remote_copy(
             src_ref=landed,
@@ -218,6 +222,8 @@
             dst = block(4 * n + m)
             side[n, j] = (wire.put(at(slot(q, places[j], co), 0, rows), dst, {"core": co}), dst)
 
+    yield
+
     def before(n, q):
         def wait(j):
             ticket, dst = side[n, j]
@@ -246,46 +252,51 @@
     xl = lax.axis_index("xl")
     z, zp, zm, z2 = near("z")
     xo = 1 - xl
-    half = rows // 2
+    cut = rows * 3 // 8
+    left = rows - cut
 
     def slot(j, q):
         return j * 2 + q
 
     def block(k, count=1):
-        return land.at[pl.ds(k * half, count * half)]
+        return land.at[pl.ds(k * cut, count * cut)]
+
+    def lower(k, count=1):
+        return land.at[pl.ds(7 * cut + k * left, count * left)]
 
     places = {0: z, 1: zp, 2: z2, 3: zm}
     side = {}
     for m, j in enumerate((2, 1, 3, 0)):
-        side[j] = (wire.put(at(slot(places[j], xo), 0, half), block(m), {"xl": xo}), block(m))
+        side[j] = (wire.put(at(slot(places[j], xo), 0, cut), block(m), {"xl": xo}), block(m))
 
     def wait(j):
         ticket, dst = side[j]
         wire.got(ticket, dst)
-        add_to(at(slot(places[j], xl), 0, half), dst)
+        add_to(at(slot(places[j], xl), 0, cut), dst)
 
     sent = []
 
     def far():
         yield from ring_scatter(
-            wire, at, lambda j: slot(j, xo), "z", half, half, block(4, 3)
+            wire, at, lambda j: slot(j, xo), "z", cut, left, lower(0, 3)
         )
-        sent.append(wire.put(at(slot(z, xo), half, half), block(13), {"xl": xo}))
+        sent.append(wire.put(at(slot(z, xo), cut, left), lower(6), {"xl": xo}))
 
     yield from together(
         far(),
-        ring_scatter(wire, at, lambda j: slot(j, xl), "z", half, half, block(7, 3)),
-        ring_scatter(wire, at, lambda j: slot(j, xl), "z", 0, half, block(10, 3), wait),
+        ring_scatter(wire, at, lambda j: slot(j, xl), "z", cut, left, lower(3, 3)),
+        ring_scatter(wire, at, lambda j: slot(j, xl), "z", 0, cut, block(4, 3), wait),
     )
-    wire.got(sent[0], block(13))
-    add_to(at(slot(z, xl), half, half), block(13))
+    wire.got(sent[0], lower(6))
+    add_to(at(slot(z, xl), cut, left), lower(6))
 
 
 def gather_head(wire, at, rows):
     xl = lax.axis_index("xl")
     z, zp, zm, z2 = near("z")
     xo = 1 - xl
-    half = rows // 2
+    cut = rows * 3 // 8
+    left = rows - cut
     up, down, across = {"z": zp}, {"z": zm}, {"xl": xo}
 
     def slot(j, q):
@@ -294,7 +305,7 @@
     def pass_on(s, first, count, to):
         return wire.put(at(s, first, count), at(s, first, count), to)
 
-    def ring(q, first, each=None):
+    def ring(q, first, half, each=None):
         h = half // 2
         tell = each or (lambda j: None)
         a = pass_on(slot(z, q), first, half, up)
@@ -315,17 +326,17 @@
     side = []
 
     def tell(j):
-        side.append((pass_on(slot(j, xl), 0, half, across), slot(j, xo)))
-
-    t_x = pass_on(slot(z, xl), half, half, across)
+        side.append((pass_on(slot(j, xl), 0, cut, across), slot(j, xo)))
+
+    t_x = pass_on(slot(z, xl), cut, left, across)
 
     def far():
-        wire.got(t_x, at(slot(z, xo), half, half))
-        yield from ring(xo, half)
-
-    yield from together(ring(xl, 0, tell), ring(xl, half), far())
+        wire.got(t_x, at(slot(z, xo), cut, left))
+        yield from ring(xo, cut, left)
+
+    yield from together(ring(xl, 0, cut, tell), ring(xl, cut, left), far())
     for ticket, s in side:
-        wire.got(ticket, at(s, 0, half))
+        wire.got(ticket, at(s, 0, cut))
 
 
 ANY = pl.BlockSpec(memory_space=pl.ANY)
@@ -535,7 +546,10 @@
     return query_grad.astype(BF16)
 
 
-def opening(r, wire, copies, work):
+WIRES = 120
+
+
+def opening(r, wire, copies, rest, work):
     rows, depth = r.mid.shape
 
     def product(out, left, right, how, *numbers):
@@ -567,6 +581,8 @@
         r.logs[...] = -rate[:, :1] * tall
 
     def states():
+        for copy in rest:
+            copy.wait()
         arow, acol = log_decays(r.logs[...])
         total = arow[0][:, RC - 1 :] + arow[1][:, RC - 1 :]
         here = seq_index()
@@ -616,24 +632,29 @@
         src = r.wkv.at[rows, pl.ds(pl.multiple_of(c * E, E), E)]
         tickets.append((wire.put(src, mine(me, c), {"z": a, "xl": b}), ca * 2 + cb))
     yield
+    yield
     for ticket, slot in tickets:
         wire.got(ticket, mine(slot, c))
         side.append((wire.put(mine(slot, c), mine(slot, c), {"core": 1 - c}), slot))
-        yield
+    yield
+    yield
+    yield
+    yield
+    yield
     for ticket, slot in side:
         wire.got(ticket, mine(slot, 1 - c))
 
 
-def closing(r, wire, run_states):
+def closing(r, wire):
     rows, depth = r.acc.shape
     share = depth // 8
     heads = r.ret_query.shape[1] // E
     me, here = head_index(), seq_index()
-    kv_at = by_rows(r.kv_all, rows, 4)
+    kv_at = by_rows(r.kv_all, rows, 16)
     w_rows = depth // 16
     w_at = by_rows(r.w_sum, w_rows)
     s_rows = heads * E
-    s_at = by_rows(r.grads, s_rows)
+    c_half = s_rows // 2
     arow, acol = log_decays(r.logs[...])
     t = lax.broadcasted_iota(jnp.int32, (RC, RC), 0)
     s = lax.broadcasted_iota(jnp.int32, (RC, RC), 1)
@@ -676,10 +697,11 @@
     next(run_keys)
     for k in range(0, depth, share):
         r.acc[:, k : k + share] = dot_last(r.q_grad[...], r.wq0[k : k + share]).astype(BF16)
-    wire.work = [lambda h=h: arriving(h) for h in range(heads)]
-    wire.work += [lambda h=h, c=c: prepare(h, c) for h, c in pieces]
+    work = [lambda h=h: arriving(h) for h in range(heads)]
+    work += [lambda h=h, c=c: prepare(h, c) for h, c in pieces]
+    wire.planned(work, {2: 9})
     m_at = by_columns(r.acc, share)
-    finish(together(scatter_head(wire, m_at, rows, r.land), run_keys))
+    finish(together(run_keys, scatter_head(wire, m_at, rows, r.land)))
     wire.idle(len(wire.work))
     own_kv = kv_at(me, 0, rows)
     gather_kv = gather_head(wire, kv_at, rows)
@@ -692,10 +714,10 @@
         w_at(here, 0, w_rows)[...] = (
             at(here, 0, w_rows)[...].astype(F32) + rest[...].astype(F32)
         ).astype(BF16)
-        yield
         yield from gather_seq(wire, w_at, w_rows)
 
     shared = sums()
+    next(shared)
     next(shared)
 
     def beside(run):
@@ -719,9 +741,10 @@
         own_grad[h, c] = dot(turned[h, c], grad_o[span, cols]) * (1.0 / E)
     for h in range(heads):
         made = own_grad[h, 0] + jnp.exp(end(h, 0)) * own_grad[h, 1]
-        r.grads[pl.ds(pl.multiple_of(here * s_rows + h * E, E), E)] = made.astype(BF16)
-    back = gather_seq(wire, s_at, s_rows)
-    next(back)
+        r.own_state[h * E : (h + 1) * E] = made.astype(BF16)
+    core = lax.axis_index("core")
+    chip = here - core
+    ticket = wire.put(r.own_state, r.side_state, {"core": 1 - core})
     inner = {}
 
     def inside(h, c):
@@ -736,15 +759,28 @@
             dot(second[h, c], g) * (1.0 / E),
         )
 
-    wire.work = [lambda h=h, c=c: inside(h, c) for h, c in pieces]
-    beside(back)
+    wire.planned([lambda h=h, c=c: inside(h, c) for h, c in pieces], {0: 2, 1: 4})
+    wire.got(ticket, r.side_state)
+    for h in range(heads):
+        cols = slice(h * E, (h + 1) * E)
+        mine, other = r.own_state[cols].astype(F32), r.side_state[cols].astype(F32)
+        lead = r.decays[pl.ds(chip * 16 + h, 1)]
+        made = jnp.where(core == 0, mine, other) + jnp.exp(lead) * jnp.where(core == 0, other, mine)
+        r.chip_state[cols] = made.astype(BF16)
+    s_at = by_rows(r.grads, c_half)
+    s_at(here, 0, c_half)[...] = r.chip_state[pl.ds(pl.multiple_of(core * c_half, c_half), c_half)]
+    beside(gather_seq(wire, s_at, c_half))
     wire.idle(len(wire.work))
     for h in range(heads):
         now = jnp.zeros((E, E), F32)
-        for k in range(15, 0, -1):
+        for k in range(7, 0, -1):
             mine = r.grads[k * s_rows + h * E : k * s_rows + (h + 1) * E].astype(F32)
-            new = mine + jnp.exp(r.decays[k * 16 + h : k * 16 + h + 1]) * now
-            now = jnp.where(k > here, new, now)
+            both = r.decays[k * 32 + h : k * 32 + h + 1] + r.decays[k * 32 + 16 + h : k * 32 + 17 + h]
+            new = mine + jnp.exp(both) * now
+            now = jnp.where(2 * k > chip, new, now)
+        beyond = r.decays[pl.ds((chip + 1) * 16 + h, 1)]
+        new = r.side_state[h * E : (h + 1) * E].astype(F32) + jnp.exp(beyond) * now
+        now = jnp.where(core == 0, new, now)
         after[h, 1] = now.astype(BF16)
         after[h, 0] = (own_grad[h, 1] + jnp.exp(end(h, 1)) * now).astype(BF16)
     for h, c in pieces:
@@ -768,7 +804,7 @@
 
 IN_NAMES = (
     "mid_in", "second_in", "cot_in", "wk_in", "wv_in", "wq_in", "wo_in", "wr_in",
-    "ret_query", "ret_key", "ret_value", "gate", "decay_exp", "firsts",
+    "rq_in", "rk_in", "rv_in", "gate", "decay_exp", "firsts",
 )
 OUT_NAMES = ("grad_mid", "gq", "gk", "gv", "w_sum")
 
@@ -799,11 +835,17 @@
         (r.wq_in.at[0], r.wq0),
         sem=r.local.at[pl.ds(3, 5)],
     )
+    rest = bring(
+        (r.rk_in, r.ret_key),
+        (r.rv_in, r.ret_value),
+        (r.rq_in, r.ret_query),
+        sem=r.local.at[pl.ds(11, 3)],
+    )
     wire = Wire(r.send, r.recv)
     at = by_rows(r.kv, rows)
     at(here, 0, rows)[...] = dot(r.mid[...], r.wkv[...]).astype(BF16)
     answered(peers)
-    opening(r, wire, copies, wire.work)
+    opening(r, wire, copies, rest, wire.work)
     wire.work.append(lambda: fill_bias(r.bias, r.firsts, here * rows, rows, length))
 
     def clear():
@@ -866,26 +908,30 @@
     next(run_states)
     lax.fori_loop(0, heads, back(r.q1, r.g1), 0)
     next(run_states)
+    next(run_states)
     for k in range(0, depth, share):
         r.acc[:, k : k + share] = dot_last(r.q_grad[...], r.wq1[k : k + share]).astype(BF16)
+    work = []
     for h in range(heads):
-        wire.work += ahead(h, r.q0, slice(h * E, (h + 1) * E))
-    finish(
-        together(
-            head_run(wire, r.acc, r.land, r.residual, r.upstream),
-            run_states,
-        )
-    )
+        work += ahead(h, r.q0, slice(h * E, (h + 1) * E))
+    wire.planned(work, {0: 10, 16: 3, 17: 14, 34: 9})
+    for step, _ in enumerate(head_run(wire, r.acc, r.land, r.residual, r.upstream)):
+        if step in (3, 4):
+            next(run_states)
     wire.idle(len(wire.work))
     own.wait()
     late[0].wait()
     r.g0[...] = dot_last(r.upstream[...], r.wo[...]).astype(BF16)
     last = bring((r.wr_in, r.wo), sem=r.local.at[pl.ds(10, 1)])
+    finish(run_states)
+    wire.drain()
+    greet(peers)
     lax.fori_loop(0, heads, back(r.q0, r.g0), 0)
     r.acc_k[...] = r.total[...].astype(BF16)
     last[0].wait()
-    wire.drain()
-    closing(r, wire, run_states)
+    answered(peers)
+    wire.used = 0
+    closing(r, wire)
 
 
 def whole(number, *operands):
@@ -895,6 +941,9 @@
     length = 16 * rows
     shape = jax.ShapeDtypeStruct
     scratch = {
+        "ret_query": pltpu.VMEM((rows, wide), BF16),
+        "ret_key": pltpu.VMEM((rows, wide), BF16),
+        "ret_value": pltpu.VMEM((rows, wide), BF16),
         "mid": pltpu.VMEM((rows, depth), BF16),
         "second": pltpu.VMEM((rows, depth), BF16),
         "residual": pltpu.VMEM((rows, depth), BF16),
@@ -924,10 +973,13 @@
         "land_k": pltpu.VMEM((15 * rows, rows), BF16),
         "kv_all": pltpu.VMEM((8 * rows, 2 * E), BF16),
         "w_land": pltpu.VMEM((15 * depth // 16, 2 * E), BF16),
-        "grads": pltpu.VMEM((16 * wide, E), BF16),
-        "local": pltpu.SemaphoreType.DMA((11,)),
-        "send": pltpu.SemaphoreType.DMA((320,)),
-        "recv": pltpu.SemaphoreType.DMA((320,)),
+        "grads": pltpu.VMEM((8 * wide, E), BF16),
+        "own_state": pltpu.VMEM((wide, E), BF16),
+        "side_state": pltpu.VMEM((wide, E), BF16),
+        "chip_state": pltpu.VMEM((wide, E), BF16),
+        "local": pltpu.SemaphoreType.DMA((14,)),
+        "send": pltpu.SemaphoreType.DMA((WIRES,)),
+        "recv": pltpu.SemaphoreType.DMA((WIRES,)),
     }
     names = IN_NAMES + OUT_NAMES + tuple(scratch)
     shared = {"acc": "second", "g0": "g1", "q_grad": "gq"}
@@ -946,7 +998,7 @@
             shape((rows, wide), BF16),
             shape((depth, 2 * E), BF16),
         ),
-        in_specs=[ANY] * 8 + [VMEM] * 4 + [smem] * 2,
+        in_specs=[ANY] * 11 + [VMEM] + [smem] * 2,
         out_specs=(ANY, VMEM, VMEM, VMEM, VMEM),
         scratch_shapes=list(scratch.values()),
         compiler_params=pltpu.CompilerParams(

time: 158 us -> 154 us (0.975)
  Pallas kernels: 157 us -> 153 us
    pallas_call x1, Pallas kernels: 153 us -> 149 us  [whole(): pl.pallas_call(kernel, out_shape=(shape((rows, depth), BF16), shape((rows...]
where the time goes in v3:
time: 154 us
  Pallas kernels  153 us (99%)
    pallas_call x1, Pallas kernels, whole(): pl.pallas_call(kernel, out_shape=(shape((rows, depth), BF16), shape((rows...  149 us
    pallas_call x1, Pallas kernels, hand_out(): pl.pallas_call(hand_out_kernel, out_shape=tuple((shape(a.shape, a.dtype)...  3.92 us

profile of v3, /device:TPU:1, one launch (start us, length us, event | category | flops | bytes accessed | tf_op | source)
XLA Modules:
  0.0 153.6 jit_solution(9380482892561058022)
XLA Ops:
  0.6 148.9 %shard_map.181 = (bf16[256,3072]{1,0:T(8,128)(2,1)}, bf16[256,384]{1,0:T(8,128)(2,1)}, bf16[256,384]{1,0:T(8,128)(2,1)}, bf16[256,384]{1,0:T(8,128)(2,1)}, bf16[3072,256]{1,0:T(8,128)(2,1)}) custom-call(bf16[256,3072]{1,0:T(8,128)(2,1)} %refs_0_.1, bf16[256,3072]{1,0:T(8,128)(2,1)} %refs_1_.1, bf16[256,3072]{1,0:T(8,128)(2,1)} %refs_2_.1, ...), custom_call_target="tpu_custom_call" | custom-call | tf_op jit(solution)/shard_map/pallas_call | solution.py:992
  149.5 3.9 %shard_map.182 = (bf16[256,3072]{1,0:T(8,128)(2,1)}, bf16[256,384]{1,0:T(8,128)(2,1)}, bf16[256,384]{1,0:T(8,128)(2,1)}, bf16[256,384]{1,0:T(8,128)(2,1)}, f32[3072,128]{1,0:T(8,128)}, /*index=5*/f32[3072,128]{1,0:T(8,128)}) custom-call(bf16[256,3072]{1,0:T(8,128)(2,1)} %get-tuple-element.11.refs_0_, bf16[256,384]{1,0:T(8,128)(2,1)} %get-tuple-element.12.refs_1_, ...), custom_call_target="tpu_custom_call" | custom-call | tf_op jit(solution)/shard_map/pallas_call | solution.py:456

commit v4 on v3

--- a/solution.py
+++ b/solution.py
@@ -531,19 +531,40 @@
 
 def backward(q, g, kv, raised, rounded, inverse, outputs, total):
     length = kv.shape[0]
+    now = total is not None
     delta = jnp.sum(g.astype(F32) * outputs.astype(F32), axis=1, keepdims=True)
     scaled = inverse[:, :1] * (1.0 / math.sqrt(E))
-    q_t = flipped(q).astype(BF16)
-    g_t = flipped(g).astype(BF16)
+    if now:
+        q_t = flipped(q).astype(BF16)
+        g_t = flipped(g).astype(BF16)
     query_grad = jnp.zeros(q.shape, F32)
     for k in range(0, length, CHUNK):
         at = slice(k, k + CHUNK)
         dprobs = dot_last(g, kv[at, E:])
         dscores = ((raised[:, at] * scaled) * (dprobs - delta)).astype(BF16)
         query_grad = query_grad + dot(dscores, kv[at, :E])
-        total[:E, at] = total[:E, at] + dot(q_t, dscores)
-        total[E:, at] = total[E:, at] + dot(g_t, rounded[:, at])
+        if now:
+            total[:E, at] = total[:E, at] + dot(q_t, dscores)
+            total[E:, at] = total[E:, at] + dot(g_t, rounded[:, at])
+        else:
+            raised[:, at] = dscores.astype(F32)
     return query_grad.astype(BF16)
+
+
+def later_parts(q, g, raised, rounded, total):
+    held = {}
+
+    def part(k):
+        def go():
+            if k == 0:
+                held["q"], held["g"] = flipped(q()).astype(BF16), flipped(g()).astype(BF16)
+            for at in (slice(k, k + CHUNK), slice(k + CHUNK, k + 2 * CHUNK)):
+                total[:E, at] = total[:E, at] + dot(held["q"], raised[:, at].astype(BF16))
+                total[E:, at] = total[E:, at] + dot(held["g"], rounded[:, at])
+
+        return go
+
+    return [part(k) for k in range(0, raised.shape[1], 2 * CHUNK)]
 
 
 WIRES = 120
@@ -710,7 +731,7 @@
 
     def sums():
         at = by_rows(r.wkv, w_rows)
-        rest = yield from scatter_seq(wire, at, w_rows, r.w_land)
+        rest = yield from scatter_seq(wire, at, w_rows, r.wq1.at[:, pl.ds(0, 2 * E)])
         w_at(here, 0, w_rows)[...] = (
             at(here, 0, w_rows)[...].astype(F32) + rest[...].astype(F32)
         ).astype(BF16)
@@ -790,6 +811,7 @@
             inner[h, c][0] + shrink * dot_last(rv[span, cols], after[h, c])
         ).astype(BF16)
         r.gv[span, cols] = (inner[h, c][1] + shrink * dot(rk[span, cols], after[h, c])).astype(BF16)
+    shown += bring((r.gq, r.gq_out), (r.gk, r.gk_out), (r.gv, r.gv_out), sem=r.local.at[pl.ds(1, 3)])
     finish(shared)
     for copy in shown:
         copy.wait()
@@ -806,7 +828,7 @@
     "mid_in", "second_in", "cot_in", "wk_in", "wv_in", "wq_in", "wo_in", "wr_in",
     "rq_in", "rk_in", "rv_in", "gate", "decay_exp", "firsts",
 )
-OUT_NAMES = ("grad_mid", "gq", "gk", "gv", "w_sum")
+OUT_NAMES = ("grad_mid", "gq_out", "gk_out", "gv_out", "w_sum")
 
 
 def whole_kernel(names, *refs):
@@ -893,12 +915,12 @@
             item()
         return 0
 
-    def back(q, g):
+    def back(q, g, total):
         def go(h, _):
             cols = wide(h)
             r.q_grad[:, cols] = backward(
                 q[:, cols], g[:, cols], r.kv, r.raised.at[h], r.rounded.at[h], r.inverse.at[h],
-                r.outputs[:, cols], r.total,
+                r.outputs[:, cols], total,
             )
             return 0
 
@@ -906,15 +928,23 @@
 
     lax.fori_loop(0, heads, upper, 0)
     next(run_states)
-    lax.fori_loop(0, heads, back(r.q1, r.g1), 0)
+    lax.fori_loop(0, heads, back(r.q1, r.g1, None), 0)
     next(run_states)
     next(run_states)
     for k in range(0, depth, share):
         r.acc[:, k : k + share] = dot_last(r.q_grad[...], r.wq1[k : k + share]).astype(BF16)
     work = []
     for h in range(heads):
-        work += ahead(h, r.q0, slice(h * E, (h + 1) * E))
-    wire.planned(work, {0: 10, 16: 3, 17: 14, 34: 9})
+        cols = slice(h * E, (h + 1) * E)
+        work += later_parts(
+            lambda cols=cols: r.q1[:, cols],
+            lambda cols=cols: r.g1[:, cols],
+            r.raised.at[h], r.rounded.at[h], r.total,
+        )
+        work += ahead(h, r.q0, cols)
+    wire.planned(
+        work, {0: 12, 5: 2, 7: 2, 9: 2, 11: 2, 13: 2, 15: 2, 16: 4, 17: 14, 34: 6}
+    )
     for step, _ in enumerate(head_run(wire, r.acc, r.land, r.residual, r.upstream)):
         if step in (3, 4):
             next(run_states)
@@ -926,7 +956,7 @@
     finish(run_states)
     wire.drain()
     greet(peers)
-    lax.fori_loop(0, heads, back(r.q0, r.g0), 0)
+    lax.fori_loop(0, heads, back(r.q0, r.g0, r.total), 0)
     r.acc_k[...] = r.total[...].astype(BF16)
     last[0].wait()
     answered(peers)
@@ -944,6 +974,7 @@
         "ret_query": pltpu.VMEM((rows, wide), BF16),
         "ret_key": pltpu.VMEM((rows, wide), BF16),
         "ret_value": pltpu.VMEM((rows, wide), BF16),
+        "gq": pltpu.VMEM((rows, wide), BF16),
         "mid": pltpu.VMEM((rows, depth), BF16),
         "second": pltpu.VMEM((rows, depth), BF16),
         "residual": pltpu.VMEM((rows, depth), BF16),
@@ -972,7 +1003,6 @@
         "acc_k": pltpu.VMEM((2 * E, length), BF16),
         "land_k": pltpu.VMEM((15 * rows, rows), BF16),
         "kv_all": pltpu.VMEM((8 * rows, 2 * E), BF16),
-        "w_land": pltpu.VMEM((15 * depth // 16, 2 * E), BF16),
         "grads": pltpu.VMEM((8 * wide, E), BF16),
         "own_state": pltpu.VMEM((wide, E), BF16),
         "side_state": pltpu.VMEM((wide, E), BF16),
@@ -982,7 +1012,7 @@
         "recv": pltpu.SemaphoreType.DMA((WIRES,)),
     }
     names = IN_NAMES + OUT_NAMES + tuple(scratch)
-    shared = {"acc": "second", "g0": "g1", "q_grad": "gq"}
+    shared = {"acc": "second", "g0": "g1", "q_grad": "gq", "gk": "q1", "gv": "q0"}
 
     def kernel(*refs):
         again = [refs[names.index(name)] for name in shared.values()]
@@ -999,7 +1029,7 @@
             shape((depth, 2 * E), BF16),
         ),
         in_specs=[ANY] * 11 + [VMEM] + [smem] * 2,
-        out_specs=(ANY, VMEM, VMEM, VMEM, VMEM),
+        out_specs=(ANY, ANY, ANY, ANY, VMEM),
         scratch_shapes=list(scratch.values()),
         compiler_params=pltpu.CompilerParams(
             collective_id=number, has_side_effects=True, vmem_limit_bytes=67043328

time: 154 us -> 153 us (level)
  no operation moved by 1% of the time
where the time goes in v4:
time: 153 us
  Pallas kernels  152 us (99%)
    pallas_call x1, Pallas kernels, whole(): pl.pallas_call(kernel, out_shape=(shape((rows, depth), BF16), shape((rows...  148 us
    pallas_call x1, Pallas kernels, hand_out(): pl.pallas_call(hand_out_kernel, out_shape=tuple((shape(a.shape, a.dtype)...  3.92 us

profile of v4, /device:TPU:1, one launch (start us, length us, event | category | flops | bytes accessed | tf_op | source)
XLA Modules:
  0.0 152.7 jit_solution(9502362714758537457)
XLA Ops:
  0.6 147.9 %shard_map.181 = (bf16[256,3072]{1,0:T(8,128)(2,1)}, bf16[256,384]{1,0:T(8,128)(2,1)}, bf16[256,384]{1,0:T(8,128)(2,1)}, bf16[256,384]{1,0:T(8,128)(2,1)}, bf16[3072,256]{1,0:T(8,128)(2,1)}) custom-call(bf16[256,3072]{1,0:T(8,128)(2,1)} %refs_0_.1, bf16[256,3072]{1,0:T(8,128)(2,1)} %refs_1_.1, bf16[256,3072]{1,0:T(8,128)(2,1)} %refs_2_.1, ...), custom_call_target="tpu_custom_call" | custom-call | tf_op jit(solution)/shard_map/pallas_call | solution.py:1022
  148.6 3.9 %shard_map.182 = (bf16[256,3072]{1,0:T(8,128)(2,1)}, bf16[256,384]{1,0:T(8,128)(2,1)}, bf16[256,384]{1,0:T(8,128)(2,1)}, bf16[256,384]{1,0:T(8,128)(2,1)}, f32[3072,128]{1,0:T(8,128)}, /*index=5*/f32[3072,128]{1,0:T(8,128)}) custom-call(bf16[256,3072]{1,0:T(8,128)(2,1)} %get-tuple-element.11.refs_0_, bf16[256,384]{1,0:T(8,128)(2,1)} %get-tuple-element.12.refs_1_, ...), custom_call_target="tpu_custom_call" | custom-call | tf_op jit(solution)/shard_map/pallas_call | solution.py:456
